TPU v7x, 256 devices: a whole 4x4x8 slice. The times are simulated.
256 devices in a mesh: role: 2 (over core), wide: 8 (over x_hi, y), tp: 16 (over z, x_lo).
Axes of the slice: x: 4 (x_hi: 2, x_lo: 2; x = x_hi * 2 + x_lo), y: 4, z: 8, core: 2. Of those that a mesh axis runs over, the one named last changes fastest.
Arguments:
- normed: bfloat16 [4096, 4096], P('wide', ('role', 'tp')), may hold values from -0.29882812 to 0.29882812
- queries: bfloat16 [4096, 4096], P('wide', 'tp'), may hold values from -4 to 4
- keys: bfloat16 [4096, 1024], P('wide'), may hold values from -4 to 4
- values: bfloat16 [4096, 1024], P('wide'), may hold values from -6 to 6
- attn_out: bfloat16 [4096, 4096], P('wide', 'tp'), may hold values from -0.29882812 to 0.29882812
- row_logsumexp: float32 [32, 4096], P('tp'), as said below
- out_grad: bfloat16 [4096, 4096], P('wide', ('role', 'tp')), may hold values from -6 to 6
- out_weight: bfloat16 [4096, 4096], P('tp'), may hold values from -0.09375 to 0.09375
- qkv_weight: bfloat16 [4096, 6144], P(('role', 'tp')), may hold values from -0.09375 to 0.09375
- documents: int32 [4096], replicated, may hold values from 0 to 2, as said below
- tasks: int32 [8, 16, 2], replicated, may hold values from -1 to 15, as said below
Outputs:
- normed_grad: bfloat16 [4096, 4096], P('wide', ('role', 'tp'))
- out_weight_grad: bfloat16 [4096, 4096], P('tp', ('role', 'wide'))
- qkv_weight_grad: bfloat16 [4096, 6144], P(('role', 'tp'), 'wide')
Inputs may be any that keep to these rules, and one draw needn't show every extreme that they name: `documents`: document numbers never fall along the tokens, and every number from 0 to 2 is used. `tasks`: row s lists in its first slots the query blocks of server s, in [s, j, 0], followed by slots holding -1 in both places; every query block from 0 to 15 stands in exactly one slot of the table; [s, j, 1] is the block holding the first token of the document of the query block's first token. row_logsumexp[h, i] is the logarithm of the sum, over the tokens j that token i may attend, of exp(scores[h, i, j]) as computed from queries and keys.
All inputs are finite; a program needn't handle non-finite values.
Results may differ from a plain program's by a relative error of at most 0.018.
Values may be sent and summed in bfloat16 or wider, within the bound.
A program may use at most 128 MiB of HBM per device.

v0:
```python
import jax
import jax.numpy as jnp
from jax import lax
from jax.sharding import PartitionSpec as P

D = 4096
QUERY_HEADS = 32
KEY_VALUE_HEADS = 8
HEAD_SIZE = 128


def cut_along(shard, dim, length):
    before, after = (shard.shape[:dim], shard.shape[dim + 1 :])
    return jnp.moveaxis(shard.reshape(*before, length, -1, *after), dim, 0)


def sum_at_owner(shard, axis, dim):
    tiles = cut_along(shard, dim, lax.axis_size(axis))
    arrived = lax.all_to_all(tiles, axis, split_axis=0, concat_axis=0, tiled=True)
    return arrived.astype(jnp.float32).sum(axis=0)


def in_one_piece(arrays, axis, dim, along):
    both = jnp.concatenate(arrays, axis=along)
    out, at, done = (lax.all_gather(both, axis, axis=dim, tiled=True), 0, [])
    for a in arrays:
        done.append(lax.slice_in_dim(out, at, at + a.shape[along], axis=along))
        at += a.shape[along]
    return tuple(done)


def local(
    normed,
    queries,
    keys,
    values,
    attn_out,
    row_logsumexp,
    out_grad,
    out_weight,
    qkv_weight,
    documents,
    tasks,
):
    role_pos = lax.axis_index("role")
    is_worker = role_pos == 0
    wide_count = lax.axis_size("wide")
    wide_pos = lax.axis_index("wide")
    tp_pos = lax.axis_index("tp")
    local_rows = normed.shape[0]
    row_halves = local_rows // 2
    head_count = queries.shape[1] // HEAD_SIZE
    pair_count = head_count // 2
    kv_count = max(1, head_count // 4)
    score_scale = HEAD_SIZE ** (-0.5)
    total_rows = wide_count * local_rows
    block_count = tasks.shape[1]
    full_grad = lax.all_gather(out_grad, ("role", "tp"), axis=1, tiled=True)
    grad_half = lax.dynamic_slice_in_dim(full_grad, role_pos * (D // 2), D // 2, 1)
    out_part = lax.dot_general(
        attn_out, grad_half, (((0,), (0,)), ((), ())), preferred_element_type=jnp.float32
    )
    out_sum = sum_at_owner(out_part.astype(jnp.bfloat16), "wide", 1)

    def worker_side():
        return lax.dot_general(
            full_grad, out_weight, (((1,), (1,)), ((), ())), preferred_element_type=jnp.float32
        ).astype(jnp.bfloat16)

    def server_side():
        return queries

    first_piece = lax.cond(is_worker, worker_side, server_side)
    kv_start = tp_pos * head_count // 4 * HEAD_SIZE
    key_cols = lax.dynamic_slice_in_dim(keys, kv_start, kv_count * HEAD_SIZE, 1)
    value_cols = lax.dynamic_slice_in_dim(values, kv_start, kv_count * HEAD_SIZE, 1)
    kv_piece = jnp.where(is_worker, key_cols, value_cols)
    out_piece = lax.dynamic_slice_in_dim(
        attn_out, role_pos * pair_count * HEAD_SIZE, pair_count * HEAD_SIZE, 1
    )
    gathered = in_one_piece((first_piece, kv_piece, out_piece), ("role", "wide"), 0, 1)
    grad_all = gathered[0][:total_rows]
    query_all = gathered[0][total_rows:]
    key_all = gathered[1][:total_rows]
    value_all = gathered[1][total_rows:]
    output_all = gathered[2].reshape(2, total_rows, pair_count, HEAD_SIZE)
    delta_all = jnp.einsum(
        "irpd,ripd->rpi",
        grad_all.reshape(total_rows, 2, pair_count, HEAD_SIZE),
        output_all,
        preferred_element_type=jnp.float32,
    ).reshape(pair_count, 2, total_rows)
    lse_all = row_logsumexp.reshape(pair_count, 2, total_rows)

    def tile(block_q, block_k, query_grad, kv_acc):
        offsets = jnp.arange(row_halves, dtype=jnp.int32)
        query_pos = block_q * row_halves + offsets
        key_pos = block_k * row_halves + offsets
        query_rows = lax.dynamic_slice_in_dim(
            query_all, block_q * row_halves, row_halves, 0
        ).reshape(row_halves, pair_count, 2, HEAD_SIZE)
        grad_rows = lax.dynamic_slice_in_dim(grad_all, block_q * row_halves, row_halves, 0).reshape(
            row_halves, pair_count, 2, HEAD_SIZE
        )
        key_rows = lax.dynamic_slice_in_dim(key_all, block_k * row_halves, row_halves, 0).reshape(
            row_halves, kv_count, HEAD_SIZE
        )
        value_rows = lax.dynamic_slice_in_dim(
            value_all, block_k * row_halves, row_halves, 0
        ).reshape(row_halves, kv_count, HEAD_SIZE)
        lse_rows = lax.dynamic_slice_in_dim(lse_all, block_q * row_halves, row_halves, 2)
        delta_rows = lax.dynamic_slice_in_dim(delta_all, block_q * row_halves, row_halves, 2)
        query_docs = lax.dynamic_slice_in_dim(documents, block_q * row_halves, row_halves, 0)
        key_docs = lax.dynamic_slice_in_dim(documents, block_k * row_halves, row_halves, 0)
        allowed = (query_docs[:, None] == key_docs[None, :]) & (
            key_pos[None, :] <= query_pos[:, None]
        )
        scores = (
            jnp.einsum("qphd,cpd->phqc", query_rows, key_rows, preferred_element_type=jnp.float32)
            * score_scale
        )
        probs = jnp.exp(jnp.where(allowed, scores - lse_rows[..., None], -jnp.inf))
        probs_low = probs.astype(jnp.bfloat16)
        value_grad = jnp.einsum(
            "phqc,qphd->cpd", probs_low, grad_rows, preferred_element_type=jnp.float32
        )
        prob_grad = jnp.einsum(
            "qphd,cpd->phqc", grad_rows, value_rows, preferred_element_type=jnp.float32
        )
        score_grad = (probs * (prob_grad - delta_rows[..., None]) * score_scale).astype(
            jnp.bfloat16
        )
        query_tile = jnp.einsum(
            "phqc,cpd->qphd", score_grad, key_rows, preferred_element_type=jnp.float32
        )
        query_grad = query_grad + query_tile.reshape(row_halves, head_count * HEAD_SIZE)
        key_grad = jnp.einsum(
            "phqc,qphd->cpd", score_grad, query_rows, preferred_element_type=jnp.float32
        )
        tile_kv = jnp.concatenate([key_grad, value_grad], axis=2).reshape(
            row_halves, pair_count * 2 * HEAD_SIZE
        )
        target = block_k % 2 * wide_count + block_k // 2
        current = lax.dynamic_index_in_dim(kv_acc, target, 0, keepdims=False)
        kv_acc = lax.dynamic_update_index_in_dim(kv_acc, current + tile_kv, target, 0)
        return (query_grad, kv_acc)

    def empty_side():
        return (
            jnp.zeros((block_count, row_halves, head_count * HEAD_SIZE), jnp.float32),
            jnp.zeros((block_count, row_halves, pair_count * 2 * HEAD_SIZE), jnp.float32),
        )

    def attend_side():
        own_row = lax.dynamic_index_in_dim(tasks, wide_pos, 0, keepdims=False)

        def slot_turn(number, carry):
            query_acc, kv_acc = carry
            block_q = own_row[number, 0]
            valid = block_q >= 0
            safe_q = jnp.maximum(block_q, 0)
            upper = jnp.where(valid, safe_q + 1, 0)
            lower = jnp.where(valid, own_row[number, 1], 0)

            def key_turn(block_k, inner):
                return tile(safe_q, block_k, inner[0], inner[1])

            start = jnp.zeros((row_halves, head_count * HEAD_SIZE), jnp.float32)
            query_grad, kv_acc = lax.fori_loop(lower, upper, key_turn, (start, kv_acc))
            target = safe_q % 2 * wide_count + safe_q // 2
            current = lax.dynamic_index_in_dim(query_acc, target, 0, keepdims=False)
            query_acc = lax.dynamic_update_index_in_dim(query_acc, current + query_grad, target, 0)
            return (query_acc, kv_acc)

        return lax.fori_loop(0, block_count, slot_turn, empty_side())

    query_acc, kv_acc = lax.cond(is_worker, empty_side, attend_side)
    kv_flat = kv_acc.reshape(block_count * row_halves, pair_count * 2 * HEAD_SIZE)
    kv_sum = sum_at_owner(kv_flat.astype(jnp.bfloat16), ("role", "wide"), 0)
    arrived = lax.all_to_all(
        query_acc.astype(jnp.bfloat16), ("role", "wide"), split_axis=0, concat_axis=0, tiled=True
    )
    query_piece = jnp.sum(arrived.astype(jnp.float32), axis=0).astype(jnp.bfloat16)
    head_q, key_value_head = in_one_piece(
        (query_piece, kv_sum.astype(jnp.bfloat16)), ("role", "tp"), 1, 0
    )
    query_grads = head_q.reshape(row_halves, 2, QUERY_HEADS * HEAD_SIZE)
    grouped_queries = jnp.sum(
        key_value_head.reshape(row_halves, 2, KEY_VALUE_HEADS, 2, 2 * HEAD_SIZE).astype(
            jnp.float32
        ),
        axis=3,
    ).astype(jnp.bfloat16)
    key_gradients = grouped_queries[..., :HEAD_SIZE].reshape(
        row_halves, 2, KEY_VALUE_HEADS * HEAD_SIZE
    )
    value_gradients = grouped_queries[..., HEAD_SIZE:].reshape(
        row_halves, 2, KEY_VALUE_HEADS * HEAD_SIZE
    )
    qkv_grads = jnp.concatenate([query_grads, key_gradients, value_gradients], axis=2)
    normed_grad = jnp.einsum(
        "irc,nc->rin", qkv_grads, qkv_weight, preferred_element_type=jnp.float32
    )
    normed_grad = normed_grad.reshape(local_rows, qkv_weight.shape[0]).astype(jnp.bfloat16)
    qkv_part = jnp.einsum(
        "rin,irc->nc",
        normed.reshape(2, row_halves, normed.shape[1]),
        qkv_grads,
        preferred_element_type=jnp.float32,
    )
    qkv_sum = sum_at_owner(qkv_part.astype(jnp.bfloat16), "wide", 1)
    return (normed_grad, out_sum.astype(jnp.bfloat16), qkv_sum.astype(jnp.bfloat16))


def solution(mesh):
    in_specs = (
        P("wide", ("role", "tp")),
        P("wide", "tp"),
        P("wide", None),
        P("wide", None),
        P("wide", "tp"),
        P("tp", None),
        P("wide", ("role", "tp")),
        P("tp", None),
        P(("role", "tp"), None),
        P(),
        P(),
    )
    out_specs = (P("wide", ("role", "tp")), P("tp", ("role", "wide")), P(("role", "tp"), "wide"))
    return jax.shard_map(local, mesh=mesh, in_specs=in_specs, out_specs=out_specs, check_vma=False)
```

profile of v0, /device:TPU:23, one launch (start us, length us, event | category | flops | bytes accessed | tf_op | source)
XLA Modules:
  0.0 612.8 jit_solution(3537214650441579339)
XLA Ops:
  10.3 75.2 %all-gather.4.cloned.1.call-done = bf16[512,4096]{1,0:T(8,128)(2,1)} async-done(((bf16[512,128]{1,0:T(8,128)(2,1)}), bf16[512,4096]{1,0:T(8,128)(2,1)}) %all-gather.4.cloned.1.call-update) | async-done | bytes 4194320 | tf_op jit(solution)/shard_map/all_gather | solution.py:58
  87.5 79.8 %all-gather.6.cloned.1.call-done = bf16[8192,512]{0,1:T(8,128)(2,1)} async-done(((bf16[512,512]{0,1:T(8,128)(2,1)}), bf16[8192,512]{0,1:T(8,128)(2,1)}) %all-gather.6.cloned.1.call-update) | async-done | bytes 8388624 | tf_op jit(solution)/shard_map/all_gather | solution.py:25
  170.5 4.1 convert.5
  174.5 214.2 %conditional.3 = (f32[16,256,256]{1,2,0:T(8,128)}, f32[16,256,256]{1,2,0:T(8,128)}) conditional(s32[]{:T(128)} %convert_element_type.57, (s32[]{:T(128)}, s32[8,16,2]{1,2,0:T(2,128)}, s32[4096]{0:T(1024)}, bf16[8192,512]{0,1:T(8,128)(2,1)}, f32[2,4096]{1,0:T(2,128)}, /*index=5*/bf16[4096,256]{0,1:T(8,128)(2,1)}, f32[2,4096,128]{1,2,0:T(8,128)}, ...), branch_computations={%region_2.7_spmd.clone, %region_7.8_spmd} | conditional | flops 172417568 | bytes 72474416 | solution.py:177
  178.4 4.5 reshape.193
  182.8 6.8 %fusion.23 = f32[2,4096]{1,0:T(2,128)S(1)} fusion(bf16[2,4096,128]{1,0,2:T(2,128)(2,1)} %reshape.193, f32[2,4096,128]{1,2,0:T(8,128)} %get-tuple-element.631), kind=kLoop, calls=%fused_computation.43 | loop fusion | flops 3137536 | bytes 6324224 | tf_op jit(solution)/shard_map/irpd,ripd->rpi/dot_general | solution.py:87
  192.8 11.6 %copy.83 = bf16[8192,512]{1,0:T(8,128)(2,1)} copy(bf16[8192,512]{0,1:T(8,128)(2,1)} %get-tuple-element.632) | data formatting | bytes 16777216 | tf_op jit(solution)/shard_map
  205.7 11.6 %copy.82 = bf16[8192,512]{1,0:T(8,128)(2,1)} copy(bf16[8192,512]{0,1:T(8,128)(2,1)} %get-tuple-element.632) | data formatting | bytes 16777216 | tf_op jit(solution)/shard_map
  224.5 164.3 %while.56 = (s32[]{:T(128)}, f32[16,256,256]{1,2,0:T(8,128)}, f32[16,256,256]{1,2,0:T(8,128)}, s32[16,2]{0,1:T(2,128)S(1)}, s32[4096]{0:T(1024)}, /*index=5*/bf1...) while((s32[]{:T(128)}, f32[16,256,256]{1,2,0:T(8,128)}, ...), condition=%wide.region_6.6_spmd, body=%wide.region_3.5_spmd.sunk | while | flops 169280032 | bytes 7429371 | solution.py:175
  230.5 33.1 %while.57 = (s32[]{:T(128)}, f32[256,256]{0,1:T(8,128)S(1)}, f32[16,256,256]{1,2,0:T(8,128)}, s32[]{:T(128)}, bf16[4096,128]{1,0:T(8,128)(2,1)}, /*index=5*/s32[...) while((s32[]{:T(128)}, f32[256,256]{0,1:T(8,128)S(1)}, ...), condition=%wide.region_5.4_spmd, body=%wide.region_4.3_spmd.sunk | while | flops 169214464 | bytes 5321220 | solution.py:169
  270.5 22.1 %while.57 = (s32[]{:T(128)}, f32[256,256]{0,1:T(8,128)S(1)}, f32[16,256,256]{1,2,0:T(8,128)}, s32[]{:T(128)}, bf16[4096,128]{1,0:T(8,128)(2,1)}, /*index=5*/s32[...) while((s32[]{:T(128)}, f32[256,256]{0,1:T(8,128)S(1)}, ...), condition=%wide.region_5.4_spmd, body=%wide.region_4.3_spmd.sunk | while | flops 169214464 | bytes 5321220 | solution.py:169
  392.5 15.9 %all-to-all-start = ((bf16[16,256,256]{1,2,0:T(8,128)(2,1)}), bf16[16,256,256]{1,2,0:T(8,128)(2,1)}, u32[]{:S(2)}, u32[]{:S(2)}) async-start(bf16[16,256,256]{1,2,0:T(8,128)(2,1)} %convert_element_type.58), calls=%async_computation | async-start | bytes 4194304 | tf_op jit(solution)/shard_map/all_to_all | solution.py:180
  412.2 21.7 %all-to-all-done = bf16[16,256,256]{1,2,0:T(8,128)(2,1)} async-done(((bf16[16,256,256]{1,2,0:T(8,128)(2,1)}), bf16[16,256,256]{1,2,0:T(8,128)(2,1)}, u32[]{:S(2)}, u32[]{:S(2)}) %all-to-all-start) | async-done | bytes 2097184 | tf_op jit(solution)/shard_map/all_to_all | solution.py:180
  433.9 8.6 %all-to-all-start.1 = ((bf16[16,256,256]{1,2,0:T(8,128)(2,1)}), bf16[16,256,256]{1,2,0:T(8,128)(2,1)}, u32[]{:S(2)}, u32[]{:S(2)}) async-start(bf16[16,256,256]{1,2,0:T(8,128)(2,1)} %convert_element_type.59), calls=%async_computation.1 | async-start | bytes 4194304 | tf_op jit(solution)/shard_map/all_to_all | solution.py:19
  444.6 23.6 %all-to-all-done.1 = bf16[16,256,256]{1,2,0:T(8,128)(2,1)} async-done(((bf16[16,256,256]{1,2,0:T(8,128)(2,1)}), bf16[16,256,256]{1,2,0:T(8,128)(2,1)}, u32[]{:S(2)}, u32[]{:S(2)}) %all-to-all-start.1) | async-done | bytes 2097184 | tf_op jit(solution)/shard_map/all_to_all | solution.py:19
  474.2 7.1 %all-to-all-start.2 = ((bf16[8,256,256]{1,2,0:T(8,128)(2,1)}), bf16[8,256,256]{1,2,0:T(8,128)(2,1)S(1)}, u32[]{:S(2)}, u32[]{:S(2)}) async-start(bf16[8,256,256]{1,2,0:T(8,128)(2,1)} %bitcast.199), calls=%async_computation.2 | async-start | bytes 2097152 | tf_op jit(solution)/shard_map/all_to_all | solution.py:19
  481.3 67.7 %all-gather.8.cloned.1.call-done = bf16[512,8192]{0,1:T(8,128)(2,1)} async-done(((bf16[512,256]{0,1:T(8,128)(2,1)}), bf16[512,8192]{0,1:T(8,128)(2,1)}) %all-gather.8.cloned.1.call-update) | async-done | bytes 8388624 | tf_op jit(solution)/shard_map/all_gather | solution.py:25
  549.0 5.7 fusion.34
  554.7 6.4 %copy.60 = bf16[256,2,4096]{2,0,1:T(8,128)(2,1)} copy(bf16[256,2,4096]{0,2,1:T(8,128)(2,1)} %bitcast.194) | data formatting | bytes 8388608 | tf_op jit(solution)/shard_map/reshape | solution.py:187
  561.1 4.9 reduce_sum.62
  573.7 5.4 fusion.24
  580.1 6.6 %all-to-all-start.3 = ((bf16[8,128,768]{1,2,0:T(8,128)(2,1)}), bf16[8,128,768]{1,2,0:T(8,128)(2,1)S(1)}, u32[]{:S(2)}, u32[]{:S(2)}) async-start(bf16[8,128,768]{1,2,0:T(8,128)(2,1)} %bitcast.198), calls=%async_computation.3 | async-start | bytes 3145728 | tf_op jit(solution)/shard_map/all_to_all | solution.py:19
  588.9 6.1 fusion.28
  594.9 10.3 %all-to-all-done.3 = bf16[8,128,768]{1,2,0:T(8,128)(2,1)S(1)} async-done(((bf16[8,128,768]{1,2,0:T(8,128)(2,1)}), bf16[8,128,768]{1,2,0:T(8,128)(2,1)S(1)}, u32[]{:S(2)}, u32[]{:S(2)}) %all-to-all-start.3) | async-done | bytes 1572896 | tf_op jit(solution)/shard_map/all_to_all | solution.py:19
  (271 shorter events, 184.2 us)
Async XLA Ops:
  7.2 581.7 %copy-start = (bf16[128,6144]{1,0:T(8,128)(2,1)S(1)}, bf16[128,6144]{1,0:T(8,128)(2,1)}, u32[]{:S(2)}) copy-start(bf16[128,6144]{1,0:T(8,128)(2,1)} %param.27) | copy-start | bytes 4718596
  7.2 78.3 %all-gather.4.cloned.1.call-start = ((), (), s32[]{:S(2)}) async-start(), calls=%async_computation.4 | async-start | bytes 4325376 | tf_op jit(solution)/shard_map/all_gather | solution.py:58
  7.9 159.4 %all-gather.6.cloned.1.call-start = ((), (), s32[]{:S(2)}) async-start(), calls=%async_computation.5 | async-start | bytes 8912896 | tf_op jit(solution)/shard_map/all_gather | solution.py:25
  392.5 41.4 %all-to-all-start = ((bf16[16,256,256]{1,2,0:T(8,128)(2,1)}), bf16[16,256,256]{1,2,0:T(8,128)(2,1)}, u32[]{:S(2)}, u32[]{:S(2)}) async-start(bf16[16,256,256]{1,2,0:T(8,128)(2,1)} %convert_element_type.58), calls=%async_computation | async-start | bytes 4194304 | tf_op jit(solution)/shard_map/all_to_all | solution.py:180
  412.2 58.7 %copy-start.2 = (bf16[512,256]{1,0:T(8,128)(2,1)S(1)}, bf16[512,256]{1,0:T(8,128)(2,1)}, u32[]{:S(2)}) copy-start(bf16[512,256]{1,0:T(8,128)(2,1)} %param.23) | copy-start | bytes 786436
  433.9 34.3 %all-to-all-start.1 = ((bf16[16,256,256]{1,2,0:T(8,128)(2,1)}), bf16[16,256,256]{1,2,0:T(8,128)(2,1)}, u32[]{:S(2)}, u32[]{:S(2)}) async-start(bf16[16,256,256]{1,2,0:T(8,128)(2,1)} %convert_element_type.59), calls=%async_computation.1 | async-start | bytes 4194304 | tf_op jit(solution)/shard_map/all_to_all | solution.py:19
  442.5 106.5 %all-gather.8.cloned.1.call-start = ((), (), s32[]{:S(2)}) async-start(), calls=%async_computation.6 | async-start | bytes 8650752 | tf_op jit(solution)/shard_map/all_gather | solution.py:25
  474.2 104.8 %all-to-all-start.2 = ((bf16[8,256,256]{1,2,0:T(8,128)(2,1)}), bf16[8,256,256]{1,2,0:T(8,128)(2,1)S(1)}, u32[]{:S(2)}, u32[]{:S(2)}) async-start(bf16[8,256,256]{1,2,0:T(8,128)(2,1)} %bitcast.199), calls=%async_computation.2 | async-start | bytes 2097152 | tf_op jit(solution)/shard_map/all_to_all | solution.py:19
  565.9 7.7 %copy-start.3 = (bf16[512,128]{1,0:T(8,128)(2,1)S(1)}, bf16[512,128]{1,0:T(8,128)(2,1)}, u32[]{:S(2)}) copy-start(bf16[512,128]{1,0:T(8,128)(2,1)} %param.19) | copy-start | bytes 393220
  579.0 1.0 copy-start.1
  580.1 25.1 %all-to-all-start.3 = ((bf16[8,128,768]{1,2,0:T(8,128)(2,1)}), bf16[8,128,768]{1,2,0:T(8,128)(2,1)S(1)}, u32[]{:S(2)}, u32[]{:S(2)}) async-start(bf16[8,128,768]{1,2,0:T(8,128)(2,1)} %bitcast.198), calls=%async_computation.3 | async-start | bytes 3145728 | tf_op jit(solution)/shard_map/all_to_all | solution.py:19
Sparse Core Ops, SparseCore 0:
  9.8 75.6 all-gather.3
  88.0 79.2 all-gather.5
  471.0 77.9 all-gather.7
where the time goes:
time: 622 us; the launch traced here: 613 us
  waiting for transfers between devices  279 us (45%)
  local copies, waits for them, and re-layouts  145 us (23%)
  other arithmetic  61.1 us (10%)
  matrix products  42.8 us (7%)
  starting transfers between devices  38.4 us (6%)
  loops' own time  32.5 us (5%)
  between operations  13.9 us (2%)
    all_gather x2, waiting for transfers between devices, in_one_piece(): out, at, done = (lax.all_gather(both, axis, axis=dim, tiled=True), 0, [])  148 us
    all_gather x1, waiting for transfers between devices, local(): full_grad = lax.all_gather(out_grad, ('role', 'tp'), axis=1, tiled=True)  75.2 us
    all_to_all x3, waiting for transfers between devices, sum_at_owner(): lax.all_to_all(tiles, axis, split_axis=0, concat_axis=0, tiled=True)  33.9 us
    another operation x21, local copies, waits for them, and re-layouts  32.8 us
    another operation x1, loops' own time, attend_side(): return lax.fori_loop(0, block_count, slot_turn, empty_side())  31.7 us
    all_to_all x3, starting transfers between devices, sum_at_owner(): lax.all_to_all(tiles, axis, split_axis=0, concat_axis=0, tiled=True)  22.3 us
    all_to_all x1, waiting for transfers between devices, local(): lax.all_to_all(query_acc.astype(jnp.bfloat16), ('role', 'wide'), split_ax...  21.7 us
    dynamic_update_slice x10, other arithmetic, tile(): lax.dynamic_update_index_in_dim(kv_acc, current + tile_kv, target, 0)  17 us
  transfers between devices with their start and end apart: 7, of which 6 were waited for; matrix products, arithmetic and copies ran while one was open for 8% of the time, Pallas kernels for 0%

commit v1 on v0

v1 whole, which is shorter than its diff:
```python
import jax
import jax.numpy as jnp
from jax import lax
from jax.experimental import pallas as pl
from jax.experimental.pallas import tpu as pltpu
from jax.sharding import PartitionSpec as P

MESH = pl.DeviceIdType.MESH
D = 4096
QUERY_HEADS = 32
KEY_VALUE_HEADS = 8
HEAD_SIZE = 128
QB = 256
BLOCKS = 16
LOG2E = 1.4426950408889634
SCALE = HEAD_SIZE ** (-0.5)
NT = (((1,), (1,)), ((), ()))
TN = (((0,), (0,)), ((), ()))
NN = (((1,), (0,)), ((), ()))


def dot(a, b, dims):
    return lax.dot_general(a, b, dims, preferred_element_type=jnp.float32)


def remote(src, dst, send, recv, where):
    return pltpu.make_async_remote_copy(
        src_ref=src, dst_ref=dst, send_sem=send, recv_sem=recv, device_id=where, device_id_type=MESH
    )


def greet(places):
    barrier = pltpu.get_barrier_semaphore()
    for where in places:
        pl.semaphore_signal(barrier, inc=1, device_id=where, device_id_type=MESH)
    pl.semaphore_wait(barrier, len(places))


def place():
    r = lax.axis_index("role")
    w = lax.axis_index("wide")
    t = lax.axis_index("tp")
    return r, w, t, t // 2, t % 2


def plane_peer(w, z, xl, k):
    dx, dy = k // 4, k % 4
    peer = ((w // 4 + dx) % 2) * 4 + (w % 4 + dy) % 4
    return {"wide": peer, "tp": z * 2 + (xl if dx == 0 else 1 - xl)}


def front_kernel(
    og, ow, keys, values, ao, ag_out, kv, part, G, O, W, A, acc,
    lsem, swap_sem, x_sem, z_send, z_recv, k_send, k_recv, kp_sem, p_send, p_recv,
):
    r, w, t, z, xl = place()
    partner = {"role": 1 - r}
    inner = {"tp": z * 2 + 1 - xl}
    up = {"tp": ((z + 1) % 8) * 2 + xl}
    down = {"tp": ((z + 7) % 8) * 2 + xl}
    cols = pl.ds(pl.multiple_of(xl * 128, 128), 128)
    mine = pl.ds(pl.multiple_of(r * QB, QB), QB)
    other = pl.ds(pl.multiple_of((1 - r) * QB, QB), QB)
    heads = pl.ds(pl.multiple_of(z * 128, 128), 128)

    @pl.when(r == 0)
    def _():
        pltpu.make_async_copy(keys.at[:, heads], kv.at[r, w], lsem.at[0]).start()

    @pl.when(r == 1)
    def _():
        pltpu.make_async_copy(values.at[:, heads], kv.at[r, w], lsem.at[0]).start()

    load_own = pltpu.make_async_copy(og.at[mine, :], G.at[z, r, :, cols], lsem.at[1])
    load_own.start()
    load_w = pltpu.make_async_copy(ow, W, lsem.at[2])
    load_w.start()
    load_a = pltpu.make_async_copy(ao, A, lsem.at[3])
    load_a.start()

    peers = [plane_peer(w, z, xl, k) for k in range(1, 8)]
    greet([partner, inner, up, down] + peers)

    swap = remote(
        og.at[other, :], G.at[z, r, :, cols], swap_sem.at[0], swap_sem.at[1], partner
    )
    swap.start()
    pltpu.make_async_copy(keys.at[:, heads], kv.at[r, w], lsem.at[0]).wait()
    pushes = []
    for k in range(7):
        c = remote(kv.at[r, w], kv.at[r, w], k_send.at[k], k_recv.at[k], peers[k])
        c.start()
        pushes.append(c)
    load_own.wait()
    swap.wait_recv()
    cross = remote(
        G.at[z, :, :, cols], G.at[z, :, :, cols], x_sem.at[0], x_sem.at[1], inner
    )
    cross.start()
    load_w.wait()
    load_a.wait()
    acc[...] = jnp.zeros_like(acc)
    cross.wait_recv()

    sends = [swap, cross]
    order = []
    hands = []

    def ring(s):
        pair = []
        for d, where in ((0, up), (1, down)):
            at = (z + 8 - s) % 8 if d == 0 else (z + s) % 8
            ref = G.at[at] if s < 3 else G.at[at, d]
            c = remote(ref, ref, z_send.at[d, s], z_recv.at[d, s], where)
            c.start()
            pair.append(c)
            sends.append(c)
        return pair

    def use(at):
        k = len(order)
        hand = remote(G.at[at, 1 - r], O.at[at], p_send.at[k], p_recv.at[k], partner)
        hand.start()
        order.append(at)
        hands.append(hand)
        low = pl.ds(pl.multiple_of(at * QB, QB), QB)
        high = pl.ds(pl.multiple_of(2048 + at * QB, QB), QB)
        acc[...] += dot(G[at, 0], W[:, low], NT) + dot(G[at, 1], W[:, high], NT)

    def product(k):
        at = order[k]
        hands[k].wait_recv()
        total = dot(A[mine, :], G[at, r], TN) + dot(A[other, :], O[at], TN)
        part[at] = total.astype(part.dtype)

    pair = ring(0)
    use(z)
    for s in range(1, 4):
        pair[0].wait_recv()
        pair[1].wait_recv()
        pair = ring(s)
        use((z + 8 - s) % 8)
        use((z + s) % 8)
        if s == 2:
            product(0)
        if s == 3:
            for c in pushes:
                c.wait_recv()
            hand_kv = remote(kv.at[r], kv.at[r], kp_sem.at[0], kp_sem.at[1], partner)
            hand_kv.start()
            for k in (1, 2, 3, 4):
                product(k)
    pair[0].wait_recv()
    pair[1].wait_recv()
    use((z + 4) % 8)
    ag_out[...] = acc[...].astype(ag_out.dtype)
    for k in (5, 6, 7):
        product(k)
    hand_kv.wait_recv()
    hand_kv.wait_send()
    for c in sends + pushes + hands:
        c.wait_send()


def front(out_grad, out_weight, keys, values, attn_out):
    hbm = pl.BlockSpec(memory_space=pltpu.HBM)
    vmem = pl.BlockSpec(memory_space=pltpu.VMEM)
    dma = pltpu.SemaphoreType.DMA
    return pl.pallas_call(
        front_kernel,
        name="front",
        out_shape=(
            jax.ShapeDtypeStruct((QB, QB), jnp.bfloat16),
            jax.ShapeDtypeStruct((2, 8, 512, 128), jnp.bfloat16),
            jax.ShapeDtypeStruct((8, QB, QB), jnp.bfloat16),
        ),
        in_specs=[hbm] * 5,
        out_specs=(vmem, vmem, vmem),
        scratch_shapes=[
            pltpu.VMEM((8, 2, QB, QB), jnp.bfloat16),
            pltpu.VMEM((8, QB, QB), jnp.bfloat16),
            pltpu.VMEM((QB, D), jnp.bfloat16),
            pltpu.VMEM((512, QB), jnp.bfloat16),
            pltpu.VMEM((QB, QB), jnp.float32),
            dma((4,)), dma((2,)), dma((2,)), dma((2, 4)), dma((2, 4)),
            dma((7,)), dma((7,)), dma((2,)), dma((8,)), dma((8,)),
        ],
        compiler_params=pltpu.CompilerParams(
            collective_id=0, has_side_effects=True, vmem_limit_bytes=40 * 1024 * 1024
        ),
        cost_estimate=pl.CostEstimate(flops=2_000_000_000, bytes_accessed=20_000_000, transcendentals=0),
    )(out_grad, out_weight, keys, values, attn_out)


def first_at_least(docs, value):
    def step(_, span):
        low, high = span
        mid = (low + high) // 2
        below = docs[jnp.minimum(mid, 4095)] < value
        live = low < high
        return (
            jnp.where(live & below, mid + 1, low),
            jnp.where(live & jnp.logical_not(below), mid, high),
        )

    return lax.fori_loop(0, 13, step, (jnp.int32(0), jnp.int32(4096)))[0]


def attn_kernel(docs, q_ref, ag, ao, lse, kv, dq_out, dkv, q2, g2, dq):
    r, w, t, z, xl = place()
    block = 2 * w + r
    start_at = block * QB
    rows = pl.ds(pl.multiple_of(r * QB, QB), QB)
    second = first_at_least(docs, 1)
    third = first_at_least(docs, 2)

    def doc_start(at):
        return jnp.where(at >= third, third, jnp.where(at >= second, second, 0))

    span = pl.ds(pl.multiple_of(start_at, QB), QB)
    deltas, lses = [], []
    for h in range(2):
        hc = pl.ds(h * 128, 128)
        q2[pl.ds(h * QB, QB), :] = q_ref[rows, hc]
        g = ag[:, hc]
        g2[pl.ds(h * QB, QB), :] = g
        both = g.astype(jnp.float32) * ao[rows, hc].astype(jnp.float32)
        deltas.append(jnp.sum(both.T, axis=0, keepdims=True))
        lses.append(lse[pl.ds(h, 1), span] * LOG2E)
    delta = jnp.concatenate(deltas, axis=1)
    lse2 = jnp.concatenate(lses, axis=1)
    lane = lax.broadcasted_iota(jnp.int32, (1, 2 * QB), 1)
    q_pos = start_at + jnp.where(lane >= QB, lane - QB, lane)
    q_start = doc_start(q_pos)
    dq[...] = jnp.zeros_like(dq)
    dkv[...] = jnp.zeros_like(dkv)

    @pl.loop(doc_start(start_at) // QB, block + 1)
    def _(kb):
        k_rows = kv[0, kb]
        v_rows = kv[1, kb]
        scores = dot(k_rows, q2[...], NT)
        k_pos = kb * QB + lax.broadcasted_iota(jnp.int32, (QB, 1), 0)
        allowed = (k_pos <= q_pos) & (k_pos >= q_start)
        probs = jnp.where(allowed, jnp.exp2(scores * (SCALE * LOG2E) - lse2), 0.0)
        dv = dot(probs.astype(jnp.bfloat16), g2[...], NN)
        prob_grad = dot(v_rows, g2[...], NT)
        ds = (probs * (prob_grad - delta)).astype(jnp.bfloat16)
        dk = dot(ds, q2[...], NN) * SCALE
        dq[...] += dot(ds, k_rows, TN)
        dkv[kb // 2, kb % 2, :, 0:128] = dk.astype(jnp.bfloat16)
        dkv[kb // 2, kb % 2, :, 128:256] = dv.astype(jnp.bfloat16)

    for h in range(2):
        dq_out[:, h * 128:(h + 1) * 128] = (dq[pl.ds(h * QB, QB), :] * SCALE).astype(jnp.bfloat16)


def attend(documents, queries, attn_grad, attn_out, lse, kv):
    vmem = pl.BlockSpec(memory_space=pltpu.VMEM)
    return pl.pallas_call(
        attn_kernel,
        name="attend",
        out_shape=(
            jax.ShapeDtypeStruct((QB, QB), jnp.bfloat16),
            jax.ShapeDtypeStruct((8, 2, QB, QB), jnp.bfloat16),
        ),
        in_specs=[pl.BlockSpec(memory_space=pltpu.SMEM)] + [vmem] * 5,
        out_specs=(vmem, vmem),
        scratch_shapes=[
            pltpu.VMEM((2 * QB, 128), jnp.bfloat16),
            pltpu.VMEM((2 * QB, 128), jnp.bfloat16),
            pltpu.VMEM((2 * QB, 128), jnp.float32),
        ],
        compiler_params=pltpu.CompilerParams(vmem_limit_bytes=40 * 1024 * 1024),
        cost_estimate=pl.CostEstimate(
            flops=5_000_000_000, bytes_accessed=6_000_000, transcendentals=2_000_000
        ),
    )(documents, queries, attn_grad, attn_out, lse, kv)


def cut_along(shard, dim, length):
    before, after = (shard.shape[:dim], shard.shape[dim + 1 :])
    return jnp.moveaxis(shard.reshape(*before, length, -1, *after), dim, 0)


def sum_at_owner(shard, axis, dim):
    tiles = cut_along(shard, dim, lax.axis_size(axis))
    arrived = lax.all_to_all(tiles, axis, split_axis=0, concat_axis=0, tiled=True)
    return arrived.astype(jnp.float32).sum(axis=0)


def in_one_piece(arrays, axis, dim, along):
    both = jnp.concatenate(arrays, axis=along)
    out, at, done = (lax.all_gather(both, axis, axis=dim, tiled=True), 0, [])
    for a in arrays:
        done.append(lax.slice_in_dim(out, at, at + a.shape[along], axis=along))
        at += a.shape[along]
    return tuple(done)


def local(
    normed, queries, keys, values, attn_out, row_logsumexp, out_grad, out_weight, qkv_weight, documents, tasks
):
    row_halves = QB
    local_rows = 512
    attn_grad, kv, part = front(out_grad, out_weight, keys, values, attn_out)
    arrived = lax.all_to_all(part, "wide", split_axis=0, concat_axis=0, tiled=True)
    out_sum = arrived.astype(jnp.float32).sum(axis=0)
    query_piece, dkv = attend(
        documents, queries, attn_grad, attn_out, row_logsumexp, kv.reshape(2, BLOCKS, QB, 128)
    )
    kv_flat = dkv.transpose(1, 0, 2, 3).reshape(BLOCKS * QB, QB)
    kv_sum = sum_at_owner(kv_flat, ("role", "wide"), 0)
    head_q, key_value_head = in_one_piece(
        (query_piece, kv_sum.astype(jnp.bfloat16)), ("role", "tp"), 1, 0
    )
    query_grads = head_q.reshape(row_halves, 2, QUERY_HEADS * HEAD_SIZE)
    grouped_queries = jnp.sum(
        key_value_head.reshape(row_halves, 2, KEY_VALUE_HEADS, 2, 2 * HEAD_SIZE).astype(
            jnp.float32
        ),
        axis=3,
    ).astype(jnp.bfloat16)
    key_gradients = grouped_queries[..., :HEAD_SIZE].reshape(
        row_halves, 2, KEY_VALUE_HEADS * HEAD_SIZE
    )
    value_gradients = grouped_queries[..., HEAD_SIZE:].reshape(
        row_halves, 2, KEY_VALUE_HEADS * HEAD_SIZE
    )
    qkv_grads = jnp.concatenate([query_grads, key_gradients, value_gradients], axis=2)
    normed_grad = jnp.einsum(
        "irc,nc->rin", qkv_grads, qkv_weight, preferred_element_type=jnp.float32
    )
    normed_grad = normed_grad.reshape(local_rows, qkv_weight.shape[0]).astype(jnp.bfloat16)
    qkv_part = jnp.einsum(
        "rin,irc->nc",
        normed.reshape(2, row_halves, normed.shape[1]),
        qkv_grads,
        preferred_element_type=jnp.float32,
    )
    qkv_sum = sum_at_owner(qkv_part.astype(jnp.bfloat16), "wide", 1)
    return (normed_grad, out_sum.astype(jnp.bfloat16), qkv_sum.astype(jnp.bfloat16))


def solution(mesh):
    in_specs = (
        P("wide", ("role", "tp")),
        P("wide", "tp"),
        P("wide", None),
        P("wide", None),
        P("wide", "tp"),
        P("tp", None),
        P("wide", ("role", "tp")),
        P("tp", None),
        P(("role", "tp"), None),
        P(),
        P(),
    )
    out_specs = (P("wide", ("role", "tp")), P("tp", ("role", "wide")), P(("role", "tp"), "wide"))
    return jax.shard_map(local, mesh=mesh, in_specs=in_specs, out_specs=out_specs, check_vma=False)
```

time: 622 us -> 269 us (0.43)
  waiting for transfers between devices: 279 us -> 93.8 us
  local copies, waits for them, and re-layouts: 145 us -> 35.2 us
  Pallas kernels: 0 us -> 47.4 us
  other arithmetic: 61.1 us -> 17.7 us
  matrix products: 42.8 us -> 8.26 us
  blocking collectives: 0 us -> 34.5 us
  loops' own time: 32.5 us -> 0 us
  starting transfers between devices: 38.4 us -> 14.9 us
    all_gather x1 -> x0, waiting for transfers between devices: 75.2 us -> none  [local(): full_grad = lax.all_gather(out_grad, ('role', 'tp'), axis=1, tiled=True)]
    dynamic_slice x92 -> x0, local copies, waits for them, and re-layouts: 74.6 us -> none  [the longest x16 15.8 us: tile(): lax.dynamic_slice_in_dim(grad_all, block_q * row_halves, row_halves, 0)]
    all_gather x2 -> x1, waiting for transfers between devices: 148 us -> 82.6 us  [in_one_piece(): out, at, done = (lax.all_gather(both, axis, axis=dim, tiled=True), 0, [])]
    pallas_call x0 -> x2, Pallas kernels: none -> 47.4 us  [the longest x1 43.1 us: front(): pl.pallas_call(front_kernel, name='front', out_shape=(jax.ShapeDtypeStruc...]
    all_to_all x0 -> x1, blocking collectives: none -> 34.5 us  [sum_at_owner(): lax.all_to_all(tiles, axis, split_axis=0, concat_axis=0, tiled=True)]
    another operation x21 -> x0, local copies, waits for them, and re-layouts: 32.8 us -> none
    another operation x19 -> x0, loops' own time: 32.5 us -> none  [the longest x1 31.7 us: attend_side(): return lax.fori_loop(0, block_count, slot_turn, empty_side())]
    dot_general x51 -> x0, matrix products: 31.3 us -> none  [the longest x10 10.9 us: tile(): jnp.einsum('qphd,cpd->phqc', query_rows, key_rows, preferred_element_type...]
  transfers between devices with their start and end apart: 7 -> 3, of which waited for: 6 -> 2; matrix products, arithmetic and copies ran while one was open for 8% -> 18% of each run, Pallas kernels for 0% -> 0%
where the time goes in v1:
time: 269 us; the launch traced here: 266 us
  waiting for transfers between devices  93.8 us (35%)
  Pallas kernels  47.4 us (18%)
  local copies, waits for them, and re-layouts  35.2 us (13%)
  blocking collectives  34.5 us (13%)
  other arithmetic  17.7 us (7%)
  starting transfers between devices  14.9 us (6%)
  between operations  14.2 us (5%)
  matrix products  8.26 us (3%)
    all_gather x1, waiting for transfers between devices, in_one_piece(): out, at, done = (lax.all_gather(both, axis, axis=dim, tiled=True), 0, [])  82.6 us
    pallas_call x1, Pallas kernels, front(): pl.pallas_call(front_kernel, name='front', out_shape=(jax.ShapeDtypeStruc...  43.1 us
    all_to_all x1, blocking collectives, sum_at_owner(): lax.all_to_all(tiles, axis, split_axis=0, concat_axis=0, tiled=True)  34.5 us
    unnamed x33, local copies, waits for them, and re-layouts  13.4 us
    reduce_sum x1, other arithmetic, local(): jnp.sum(key_value_head.reshape(row_halves, 2, KEY_VALUE_HEADS, 2, 2 * HEA...  12.8 us
    all_to_all x1, waiting for transfers between devices, sum_at_owner(): lax.all_to_all(tiles, axis, split_axis=0, concat_axis=0, tiled=True)  11.2 us
    all_to_all x1, starting transfers between devices, local(): lax.all_to_all(part, 'wide', split_axis=0, concat_axis=0, tiled=True)  8.25 us
    reshape x1, local copies, waits for them, and re-layouts, local(): key_value_head.reshape(row_halves, 2, KEY_VALUE_HEADS, 2, 2 * HEAD_SIZE)  7.77 us
  transfers between devices with their start and end apart: 3, of which 2 were waited for; matrix products, arithmetic and copies ran while one was open for 18% of the time, Pallas kernels for 0%

profile of v1, /device:TPU:23, one launch (start us, length us, event | category | flops | bytes accessed | tf_op | source)
XLA Modules:
  0.0 266.0 jit_solution(1078208263287761129)
XLA Ops:
  7.2 1.7 copy-done.1
  8.9 1.2 copy-done.2
  10.2 1.2 copy-done.3
  11.4 0.9 copy-done.5
  13.2 43.1 %front.1 = (bf16[256,256]{1,0:T(8,128)(2,1)S(1)}, bf16[2,8,512,128]{3,2,1,0:T(8,128)(2,1)S(1)}, bf16[8,256,256]{2,1,0:T(8,128)(2,1)}) custom-call(bf16[512,128]{1,0:T(8,128)(2,1)S(1)} %copy-done.7, bf16[256,4096]{1,0:T(8,128)(2,1)S(1)} %copy-done.1, bf16[512,1024]{1,0:T(8,128)(2,1)S(1)} %copy-done.2, bf16[512,1024]{1,0:T(8,128)(2,1)S(1)} %copy-done.3, ...), custom_call_target="tpu_custom_call" | custom-call | flops 2000000000 | bytes 20000000 | tf_op jit(solution)/shard_map/front/pallas_call | solution.py:169
  56.4 4.3 %attend.1 = (bf16[256,256]{1,0:T(8,128)(2,1)S(1)}, bf16[8,2,256,256]{3,2,1,0:T(8,128)(2,1)S(1)}) custom-call(s32[4096]{0:T(1024)S(1)} %copy-done.9, bf16[512,256]{1,0:T(8,128)(2,1)S(1)} %copy-done.4, bf16[256,256]{1,0:T(8,128)(2,1)S(1)} %get-tuple-element.8.ag, bf16[512,256]{1,0:T(8,128)(2,1)S(1)} %copy-done.6, f32[2,4096]{1,0:T(2,128)S(1)} %copy-done.8, ...), custom_call_target="tpu_custom_call" | custom-call | flops 5000000000 | bytes 6000000 | tf_op jit(solution)/shard_map/attend/pallas_call | solution.py:260
  60.9 34.5 %all_to_all.15 = bf16[16,256,256]{2,1,0:T(8,128)(2,1)} all-to-all(bf16[16,256,256]{2,1,0:T(8,128)(2,1)S(1)} %bitcast.34), channel_id=1, replica_groups=mesh['role'=2,'wide'=8,'tp'=16] {'role','wide'}, dimensions={0} | all-to-all | bytes 4194304 | tf_op jit(solution)/shard_map/all_to_all | solution.py:288
  95.4 1.9 reduce_sum.48
  98.1 8.3 %all-to-all-start.1 = ((bf16[8,256,256]{2,1,0:T(8,128)(2,1)}), bf16[8,256,256]{2,1,0:T(8,128)(2,1)S(1)}, u32[]{:S(2)}, u32[]{:S(2)}) async-start(bf16[8,256,256]{2,1,0:T(8,128)(2,1)} %get-tuple-element.12), calls=%async_computation.1 | async-start | bytes 2097152 | tf_op jit(solution)/shard_map/all_to_all | solution.py:307
  106.3 82.6 %all-gather.2.cloned.1.call-done = bf16[512,8192]{1,0:T(8,128)(2,1)} async-done(((bf16[512,256]{1,0:T(8,128)(2,1)}), bf16[512,8192]{1,0:T(8,128)(2,1)}) %all-gather.2.cloned.1.call-update) | async-done | bytes 8388624 | tf_op jit(solution)/shard_map/all_gather | solution.py:294
  188.9 5.9 %fusion.6 = (bf16[256,8192]{1,0:T(8,128)(2,1)}, bf16[256,8192]{1,0:T(8,128)(2,1)}) fusion(bf16[512,8192]{1,0:T(8,128)(2,1)} %all-gather.2.cloned.1.call-done), kind=kLoop, calls=%fused_computation.9 | loop fusion | bytes 16777216 | tf_op jit(solution)/shard_map/slice | solution.py:296
  194.8 7.8 %reshape.31 = bf16[256,2,8,2,256]{4,3,2,1,0:T(2,128)(2,1)} reshape(bf16[256,8192]{1,0:T(8,128)(2,1)} %get-tuple-element.16) | data formatting | bytes 8388608 | tf_op jit(solution)/shard_map/reshape | solution.py:319
  202.5 12.8 %reduce_sum.49 = bf16[256,2,8,256]{3,2,1,0:T(8,128)(2,1)} reduce(bf16[256,2,8,2,256]{4,3,2,1,0:T(2,128)(2,1)} %reshape.31, bf16[]{:T(256)} %constant.5.clone.1), dimensions={3}, to_apply=%region_1.0 | reduce | flops 1048576 | bytes 6291458 | tf_op jit(solution)/shard_map/reduce_sum | solution.py:318
  215.3 3.3 %fusion.7 = (bf16[256,2,8,128]{3,2,1,0:T(8,128)(2,1)}, bf16[256,2,8,128]{3,2,1,0:T(8,128)(2,1)}) fusion(bf16[256,2,8,256]{3,2,1,0:T(8,128)(2,1)} %reduce_sum.49), kind=kLoop, calls=%fused_computation.10 | loop fusion | bytes 4194304 | tf_op jit(solution)/shard_map/slice | solution.py:327
  218.6 2.2 reshape.39
  220.8 2.2 reshape.38
  223.0 2.6 bitcast_dynamic-update-slice_fusion
  226.2 2.6 copy-done.10
  228.8 3.0 %fusion = bf16[6144,128]{1,0:T(8,128)(2,1)} fusion(bf16[256,2,6144]{2,0,1:T(8,128)(2,1)S(1)} %copy_dynamic-update-slice_fusion, bf16[2,256,128]{2,1,0:T(8,128)(2,1)S(1)} %bitcast.35), kind=kOutput, calls=%fused_computation.1 | convolution fusion | flops 806092800 | bytes 7995392 | tf_op jit(solution)/shard_map/rin,irc->nc/dot_general | solution.py:335
  231.8 1.0 copy-done.11
  232.9 6.6 %all-to-all-start.2 = ((bf16[8,128,768]{1,2,0:T(8,128)(2,1)}), bf16[8,128,768]{1,2,0:T(8,128)(2,1)S(1)}, u32[]{:S(2)}, u32[]{:S(2)}) async-start(bf16[8,128,768]{1,2,0:T(8,128)(2,1)} %bitcast.10), calls=%async_computation.2 | async-start | bytes 3145728 | tf_op jit(solution)/shard_map/all_to_all | solution.py:288
  239.5 2.1 reduce_sum.50
  241.6 5.2 %fusion.3 = bf16[256,2,128]{2,0,1:T(8,128)(2,1)} fusion(bf16[256,2,6144]{2,0,1:T(8,128)(2,1)} %copy-done.10, bf16[128,6144]{1,0:T(8,128)(2,1)S(1)} %copy-done), kind=kOutput, calls=%fused_computation.5 | convolution fusion | flops 805371904 | bytes 7995392 | tf_op jit(solution)/shard_map/irc,nc->rin/dot_general | solution.py:331
  246.8 11.2 %all-to-all-done.2 = bf16[8,128,768]{1,2,0:T(8,128)(2,1)S(1)} async-done(((bf16[8,128,768]{1,2,0:T(8,128)(2,1)}), bf16[8,128,768]{1,2,0:T(8,128)(2,1)S(1)}, u32[]{:S(2)}, u32[]{:S(2)}) %all-to-all-start.2) | async-done | bytes 1572896 | tf_op jit(solution)/shard_map/all_to_all | solution.py:288
  (33 shorter events, 3.6 us)
Async XLA Ops:
  7.2 234.4 %copy-start = (bf16[128,6144]{1,0:T(8,128)(2,1)S(1)}, bf16[128,6144]{1,0:T(8,128)(2,1)}, u32[]{:S(2)}) copy-start(bf16[128,6144]{1,0:T(8,128)(2,1)} %param.19) | copy-start | bytes 4718596
  7.2 181.7 %all-gather.2.cloned.1.call-start = ((), (), s32[]{:S(2)}) async-start(), calls=%async_computation.3 | async-start | bytes 8650752 | tf_op jit(solution)/shard_map/all_gather | solution.py:294
  7.2 1.7 copy-start.1
  8.9 1.2 copy-start.2
  10.2 1.2 copy-start.3
  11.4 0.9 copy-start.5
  12.3 0.9 copy-start.7
  13.2 43.1 %copy-start.4 = (bf16[512,256]{1,0:T(8,128)(2,1)S(1)}, bf16[512,256]{1,0:T(8,128)(2,1)}, u32[]{:S(2)}) copy-start(bf16[512,256]{1,0:T(8,128)(2,1)} %q_ref.1) | copy-start | bytes 786436
  13.2 43.1 %copy-start.6 = (bf16[512,256]{1,0:T(8,128)(2,1)S(1)}, bf16[512,256]{1,0:T(8,128)(2,1)}, u32[]{:S(2)}) copy-start(bf16[512,256]{1,0:T(8,128)(2,1)} %ao.3) | copy-start | bytes 786436
  13.2 43.1 %copy-start.8 = (f32[2,4096]{1,0:T(2,128)S(1)}, f32[2,4096]{1,0:T(2,128)}, u32[]{:S(2)}) copy-start(f32[2,4096]{1,0:T(2,128)} %lse.1) | copy-start | bytes 98308
  13.2 43.1 %copy-start.9 = (s32[4096]{0:T(1024)S(1)}, s32[4096]{0:T(1024)}, u32[]{:S(2)}) copy-start(s32[4096]{0:T(1024)} %docs.1) | copy-start | bytes 49156
  98.1 133.8 %all-to-all-start.1 = ((bf16[8,256,256]{2,1,0:T(8,128)(2,1)}), bf16[8,256,256]{2,1,0:T(8,128)(2,1)S(1)}, u32[]{:S(2)}, u32[]{:S(2)}) async-start(bf16[8,256,256]{2,1,0:T(8,128)(2,1)} %get-tuple-element.12), calls=%async_computation.1 | async-start | bytes 2097152 | tf_op jit(solution)/shard_map/all_to_all | solution.py:307
  222.9 2.6 copy-start.13
  223.0 2.9 %copy-start.12 = (bf16[256,2,1024]{2,1,0:T(2,128)(2,1)S(1)}, bf16[256,2,1024]{2,1,0:T(2,128)(2,1)}, u32[]{:S(2)}) copy-start(bf16[256,2,1024]{2,1,0:T(2,128)(2,1)} %reshape.39) | copy-start | bytes 3145732
  225.6 3.2 %copy-start.14 = (bf16[512,128]{1,0:T(8,128)(2,1)S(1)}, bf16[512,128]{1,0:T(8,128)(2,1)}, u32[]{:S(2)}) copy-start(bf16[512,128]{1,0:T(8,128)(2,1)} %param.11) | copy-start | bytes 393220
  226.2 2.6 copy-start.10
  231.8 1.0 copy-start.11
  232.9 25.1 %all-to-all-start.2 = ((bf16[8,128,768]{1,2,0:T(8,128)(2,1)}), bf16[8,128,768]{1,2,0:T(8,128)(2,1)S(1)}, u32[]{:S(2)}, u32[]{:S(2)}) async-start(bf16[8,128,768]{1,2,0:T(8,128)(2,1)} %bitcast.10), calls=%async_computation.2 | async-start | bytes 3145728 | tf_op jit(solution)/shard_map/all_to_all | solution.py:288
Sparse Core Ops, SparseCore 0:
  98.2 90.6 all-gather.1

commit v2 on v1

--- a/solution.py
+++ b/solution.py
@@ -278,68 +278,305 @@
     )(documents, queries, attn_grad, attn_out, lse, kv)
 
 
-def cut_along(shard, dim, length):
-    before, after = (shard.shape[:dim], shard.shape[dim + 1 :])
-    return jnp.moveaxis(shard.reshape(*before, length, -1, *after), dim, 0)
-
-
-def sum_at_owner(shard, axis, dim):
-    tiles = cut_along(shard, dim, lax.axis_size(axis))
-    arrived = lax.all_to_all(tiles, axis, split_axis=0, concat_axis=0, tiled=True)
-    return arrived.astype(jnp.float32).sum(axis=0)
-
-
-def in_one_piece(arrays, axis, dim, along):
-    both = jnp.concatenate(arrays, axis=along)
-    out, at, done = (lax.all_gather(both, axis, axis=dim, tiled=True), 0, [])
-    for a in arrays:
-        done.append(lax.slice_in_dim(out, at, at + a.shape[along], axis=along))
-        at += a.shape[along]
-    return tuple(done)
+def back_kernel(
+    dq, dkv, normed, wq, ng_out, gw_out, QF, KF, D1, S, D2, F, FR, N, nacc, kacc,
+    lsem, d1s, d1r, d2s, d2r, x_sem, z_send, z_recv, p_send, p_recv, kx_sem, kz_send, kz_recv,
+    kp_send, kp_recv, f_send, f_recv,
+):
+    r, w, t, z, xl = place()
+    partner = {"role": 1 - r}
+    inner = {"tp": z * 2 + 1 - xl}
+    up = {"tp": ((z + 1) % 8) * 2 + xl}
+    down = {"tp": ((z + 7) % 8) * 2 + xl}
+    plane = [{"wide": (w + k // 2) % 8, "tp": z * 2 + (xl + k % 2) % 2} for k in range(1, 16)]
+    load_n = pltpu.make_async_copy(normed, N, lsem.at[0])
+    load_n.start()
+    keep = pltpu.make_async_copy(dq, QF.at[r, z, xl], lsem.at[1])
+    keep.start()
+    greet([partner, up, down] + plane)
+
+    def first(wp):
+        return remote(dkv.at[wp, 1 - r], D1.at[wp], d1s.at[wp], d1r.at[wp], partner)
+
+    @pl.loop(0, w + 1)
+    def _(i):
+        first(w - i).start()
+
+    cross = remote(dq, QF.at[r, z, xl], x_sem.at[0], x_sem.at[1], inner)
+    cross.start()
+
+    def second(wp, kind):
+        return remote(
+            S.at[wp, kind], D2.at[w, xl], d2s.at[wp, kind], d2r.at[w, xl],
+            {"wide": wp, "tp": z * 2 + kind},
+        )
+
+    def arrive(ws, xs):
+        return remote(
+            S.at[w, xl], D2.at[ws, xs], d2s.at[w, xl], d2r.at[ws, xs],
+            {"wide": ws, "tp": z * 2 + xs},
+        )
+
+    def pair_sum(wp):
+        first(wp).wait_recv()
+        both = dkv[wp, r].astype(jnp.float32) + D1[wp].astype(jnp.float32)
+        low = both.astype(jnp.bfloat16)
+        S[wp, 0] = low[:, 0:128]
+        S[wp, 1] = low[:, 128:256]
+
+    pair_sum(w)
+    second(w, 1 - xl).start()
+
+    @pl.loop(0, w)
+    def _(i):
+        wp = w - 1 - i
+        pair_sum(wp)
+        second(wp, 0).start()
+        second(wp, 1).start()
+
+    keep.wait()
+    cross.wait_recv()
+    load_n.wait()
+    nacc[...] = jnp.zeros_like(nacc)
+    sends = [cross]
+    order, hands, k_order, k_hands = [], [], [], []
+
+    def ring(buf, ss, rs, s):
+        pair = []
+        for d, where in ((0, up), (1, down)):
+            at = (z + 8 - s) % 8 if d == 0 else (z + s) % 8
+            ref = buf.at[r, at] if s < 3 else buf.at[r, at, d]
+            c = remote(ref, ref, ss.at[d, s], rs.at[d, s], where)
+            c.start()
+            pair.append(c)
+            sends.append(c)
+        return pair
+
+    def hand(buf, ss, rs, at, seen, copies):
+        c = remote(buf.at[r, at], buf.at[r, at], ss.at[len(seen)], rs.at[len(seen)], partner)
+        c.start()
+        seen.append(at)
+        copies.append(c)
+
+    def handed(buf, ss, rs, k, seen):
+        remote(buf.at[1 - r, seen[k]], buf.at[1 - r, seen[k]], ss.at[k], rs.at[k], partner).wait_recv()
+
+    def process(k):
+        handed(QF, p_send, p_recv, k, order)
+        at = order[k]
+        for x in range(2):
+            cols = pl.ds(pl.multiple_of((2 * at + x) * QB, QB), QB)
+            weight = wq[:, cols]
+            for h in range(2):
+                nacc[h] += dot(QF[h, at, x], weight, NT)
+            total = dot(N[0:QB, :], QF[0, at, x], TN) + dot(N[QB:512, :], QF[1, at, x], TN)
+            low = total.astype(jnp.bfloat16)
+            F[4 * at + 2 * x] = low[:, 0:128]
+            F[4 * at + 2 * x + 1] = low[:, 128:256]
+
+    def process_kv(k):
+        handed(KF, kp_send, kp_recv, k, k_order)
+        at = k_order[k]
+        for x in range(2):
+            cols = pl.ds(pl.multiple_of(4096 + x * 1024 + at * 128, 128), 128)
+            weight = wq[:, cols]
+            for h in range(2):
+                nacc[h] += dot(KF[h, at, x], weight, NT)
+            total = dot(N[0:QB, :], KF[0, at, x], TN) + dot(N[QB:512, :], KF[1, at, x], TN)
+            F[32 + 8 * x + at] = total.astype(jnp.bfloat16)
+
+    def chunk(wp):
+        return remote(
+            F.at[pl.ds(6 * wp, 6)], FR.at[w], f_send.at[wp], f_recv.at[w], {"wide": wp}
+        )
+
+    def chunk_in(ws):
+        return remote(F.at[pl.ds(6 * w, 6)], FR.at[ws], f_send.at[w], f_recv.at[ws], {"wide": ws})
+
+    def away(a):
+        d = (a + 8 - z) % 8
+        return jnp.minimum(d, 8 - d)
+
+    def ship(s):
+        @pl.loop(0, 5)
+        def _(wp):
+            ready = jnp.maximum(away((3 * wp) // 2), away((3 * wp + 2) // 2))
+
+            @pl.when((ready == s) & (wp != w))
+            def _():
+                chunk(wp).start()
+
+    pair = ring(QF, z_send, z_recv, 0)
+    hand(QF, p_send, p_recv, z, order, hands)
+
+    pair[0].wait_recv()
+    pair[1].wait_recv()
+    pair = ring(QF, z_send, z_recv, 1)
+    hand(QF, p_send, p_recv, (z + 7) % 8, order, hands)
+    hand(QF, p_send, p_recv, (z + 1) % 8, order, hands)
+    process(0)
+
+    arrive(w, 1 - xl).wait_recv()
+    kacc[...] = S[w, xl].astype(jnp.float32) + D2[w, 1 - xl].astype(jnp.float32)
+
+    @pl.loop(w + 1, 8)
+    def _(ws):
+        for xs in range(2):
+            arrive(ws, xs).wait_recv()
+            kacc[...] += D2[ws, xs].astype(jnp.float32)
+
+    KF[r, z, xl] = kacc[...].astype(jnp.bfloat16)
+    kcross = remote(KF.at[r, z, xl], KF.at[r, z, xl], kx_sem.at[0], kx_sem.at[1], inner)
+    kcross.start()
+    sends.append(kcross)
+    process(1)
+    process(2)
+    ship(1)
+
+    pair[0].wait_recv()
+    pair[1].wait_recv()
+    pair = ring(QF, z_send, z_recv, 2)
+    hand(QF, p_send, p_recv, (z + 6) % 8, order, hands)
+    hand(QF, p_send, p_recv, (z + 2) % 8, order, hands)
+    kcross.wait_recv()
+    k_pair = ring(KF, kz_send, kz_recv, 0)
+    hand(KF, kp_send, kp_recv, z, k_order, k_hands)
+    process(3)
+    process(4)
+    ship(2)
+
+    pair[0].wait_recv()
+    pair[1].wait_recv()
+    pair = ring(QF, z_send, z_recv, 3)
+    hand(QF, p_send, p_recv, (z + 5) % 8, order, hands)
+    hand(QF, p_send, p_recv, (z + 3) % 8, order, hands)
+    k_pair[0].wait_recv()
+    k_pair[1].wait_recv()
+    k_pair = ring(KF, kz_send, kz_recv, 1)
+    hand(KF, kp_send, kp_recv, (z + 7) % 8, k_order, k_hands)
+    hand(KF, kp_send, kp_recv, (z + 1) % 8, k_order, k_hands)
+    process(5)
+    process(6)
+    ship(3)
+    process_kv(0)
+
+    k_pair[0].wait_recv()
+    k_pair[1].wait_recv()
+    k_pair = ring(KF, kz_send, kz_recv, 2)
+    hand(KF, kp_send, kp_recv, (z + 6) % 8, k_order, k_hands)
+    hand(KF, kp_send, kp_recv, (z + 2) % 8, k_order, k_hands)
+    pair[0].wait_recv()
+    pair[1].wait_recv()
+    hand(QF, p_send, p_recv, (z + 4) % 8, order, hands)
+    process_kv(1)
+    process_kv(2)
+    process(7)
+    ship(4)
+
+    k_pair[0].wait_recv()
+    k_pair[1].wait_recv()
+    k_pair = ring(KF, kz_send, kz_recv, 3)
+    hand(KF, kp_send, kp_recv, (z + 5) % 8, k_order, k_hands)
+    hand(KF, kp_send, kp_recv, (z + 3) % 8, k_order, k_hands)
+    process_kv(3)
+    process_kv(4)
+    k_pair[0].wait_recv()
+    k_pair[1].wait_recv()
+    hand(KF, kp_send, kp_recv, (z + 4) % 8, k_order, k_hands)
+    process_kv(5)
+    process_kv(6)
+    process_kv(7)
+
+    @pl.loop(5, 8)
+    def _(wp):
+        @pl.when(wp != w)
+        def _():
+            chunk(wp).start()
+
+    for h in range(2):
+        ng_out[h * QB:(h + 1) * QB, :] = nacc[h].astype(jnp.bfloat16)
+    FR[w] = F[pl.ds(6 * w, 6)]
+
+    @pl.loop(0, 8)
+    def _(ws):
+        @pl.when(ws != w)
+        def _():
+            chunk_in(ws).wait_recv()
+
+    for j in range(6):
+        total = FR[0, j].astype(jnp.float32)
+        for ws in range(1, 8):
+            total += FR[ws, j].astype(jnp.float32)
+        gw_out[:, j * 128:(j + 1) * 128] = total.astype(jnp.bfloat16)
+
+    for c in sends + hands + k_hands:
+        c.wait_send()
+
+    @pl.loop(0, w + 1)
+    def _(wp):
+        first(wp).wait_send()
+
+    second(w, 1 - xl).wait_send()
+
+    @pl.loop(0, w)
+    def _(wp):
+        second(wp, 0).wait_send()
+        second(wp, 1).wait_send()
+
+    @pl.loop(0, 8)
+    def _(wp):
+        @pl.when(wp != w)
+        def _():
+            chunk(wp).wait_send()
+
+
+def back(dq, dkv, normed, qkv_weight):
+    vmem = pl.BlockSpec(memory_space=pltpu.VMEM)
+    hbm = pl.BlockSpec(memory_space=pltpu.HBM)
+    dma = pltpu.SemaphoreType.DMA
+    low = jnp.bfloat16
+    return pl.pallas_call(
+        back_kernel,
+        name="back",
+        out_shape=(
+            jax.ShapeDtypeStruct((512, 128), low),
+            jax.ShapeDtypeStruct((128, 768), low),
+        ),
+        in_specs=[vmem, vmem, hbm, vmem],
+        out_specs=(vmem, vmem),
+        scratch_shapes=[
+            pltpu.VMEM((2, 8, 2, QB, QB), low),
+            pltpu.VMEM((2, 8, 2, QB, 128), low),
+            pltpu.VMEM((8, QB, QB), low),
+            pltpu.VMEM((8, 2, QB, 128), low),
+            pltpu.VMEM((8, 2, QB, 128), low),
+            pltpu.VMEM((48, 128, 128), low),
+            pltpu.VMEM((8, 6, 128, 128), low),
+            pltpu.VMEM((512, 128), low),
+            pltpu.VMEM((2, QB, 128), jnp.float32),
+            pltpu.VMEM((QB, 128), jnp.float32),
+            dma((2,)), dma((8,)), dma((8,)), dma((8, 2)), dma((8, 2)), dma((2,)),
+            dma((2, 4)), dma((2, 4)), dma((8,)), dma((8,)), dma((2,)), dma((2, 4)), dma((2, 4)),
+            dma((8,)), dma((8,)), dma((8,)), dma((8,)),
+        ],
+        compiler_params=pltpu.CompilerParams(
+            collective_id=1, has_side_effects=True, vmem_limit_bytes=40 * 1024 * 1024
+        ),
+        cost_estimate=pl.CostEstimate(flops=3_000_000_000, bytes_accessed=20_000_000, transcendentals=0),
+    )(dq, dkv, normed, qkv_weight)
 
 
 def local(
     normed, queries, keys, values, attn_out, row_logsumexp, out_grad, out_weight, qkv_weight, documents, tasks
 ):
-    row_halves = QB
-    local_rows = 512
     attn_grad, kv, part = front(out_grad, out_weight, keys, values, attn_out)
     arrived = lax.all_to_all(part, "wide", split_axis=0, concat_axis=0, tiled=True)
-    out_sum = arrived.astype(jnp.float32).sum(axis=0)
-    query_piece, dkv = attend(
+    dq, dkv = attend(
         documents, queries, attn_grad, attn_out, row_logsumexp, kv.reshape(2, BLOCKS, QB, 128)
     )
-    kv_flat = dkv.transpose(1, 0, 2, 3).reshape(BLOCKS * QB, QB)
-    kv_sum = sum_at_owner(kv_flat, ("role", "wide"), 0)
-    head_q, key_value_head = in_one_piece(
-        (query_piece, kv_sum.astype(jnp.bfloat16)), ("role", "tp"), 1, 0
-    )
-    query_grads = head_q.reshape(row_halves, 2, QUERY_HEADS * HEAD_SIZE)
-    grouped_queries = jnp.sum(
-        key_value_head.reshape(row_halves, 2, KEY_VALUE_HEADS, 2, 2 * HEAD_SIZE).astype(
-            jnp.float32
-        ),
-        axis=3,
-    ).astype(jnp.bfloat16)
-    key_gradients = grouped_queries[..., :HEAD_SIZE].reshape(
-        row_halves, 2, KEY_VALUE_HEADS * HEAD_SIZE
-    )
-    value_gradients = grouped_queries[..., HEAD_SIZE:].reshape(
-        row_halves, 2, KEY_VALUE_HEADS * HEAD_SIZE
-    )
-    qkv_grads = jnp.concatenate([query_grads, key_gradients, value_gradients], axis=2)
-    normed_grad = jnp.einsum(
-        "irc,nc->rin", qkv_grads, qkv_weight, preferred_element_type=jnp.float32
-    )
-    normed_grad = normed_grad.reshape(local_rows, qkv_weight.shape[0]).astype(jnp.bfloat16)
-    qkv_part = jnp.einsum(
-        "rin,irc->nc",
-        normed.reshape(2, row_halves, normed.shape[1]),
-        qkv_grads,
-        preferred_element_type=jnp.float32,
-    )
-    qkv_sum = sum_at_owner(qkv_part.astype(jnp.bfloat16), "wide", 1)
-    return (normed_grad, out_sum.astype(jnp.bfloat16), qkv_sum.astype(jnp.bfloat16))
+    normed_grad, qkv_sum = back(dq, dkv, normed, qkv_weight)
+    out_sum = arrived.astype(jnp.float32).sum(axis=0).astype(jnp.bfloat16)
+    return normed_grad, out_sum, qkv_sum
 
 
 def solution(mesh):

time: 269 us -> 144 us (0.54); the launches traced: 266 us -> 145 us
  waiting for transfers between devices: 93.8 us -> 0.01 us
  Pallas kernels: 47.4 us -> 127 us
  blocking collectives: 34.5 us -> 0 us
  local copies, waits for them, and re-layouts: 35.2 us -> 7.25 us
  other arithmetic: 17.7 us -> 2.06 us
  between operations: 14.2 us -> 0.76 us
  matrix products: 8.26 us -> 0 us
  starting transfers between devices: 14.9 us -> 8.12 us
    all_gather x1 -> x0, waiting for transfers between devices: 82.6 us -> none  [in_one_piece(): out, at, done = (lax.all_gather(both, axis, axis=dim, tiled=True), 0, [])]
    pallas_call x0 -> x1, Pallas kernels: none -> 74.3 us  [back(): pl.pallas_call(back_kernel, name='back', out_shape=(jax.ShapeDtypeStruct(...]
    all_to_all x1 -> x0, blocking collectives: 34.5 us -> none  [sum_at_owner(): lax.all_to_all(tiles, axis, split_axis=0, concat_axis=0, tiled=True)]
    reduce_sum x4 -> x1, other arithmetic: 17 us -> 2.06 us  [local(): out_sum = arrived.astype(jnp.float32).sum(axis=0).astype(jnp.bfloat16)]
    reshape x3 -> x0, local copies, waits for them, and re-layouts: 12.2 us -> none  [the longest x1 7.77 us: local(): key_value_head.reshape(row_halves, 2, KEY_VALUE_HEADS, 2, 2 * HEAD_SIZE)]
    all_to_all x1 -> x0, waiting for transfers between devices: 11.2 us -> none  [sum_at_owner(): lax.all_to_all(tiles, axis, split_axis=0, concat_axis=0, tiled=True)]
    slice x2 -> x0, local copies, waits for them, and re-layouts: 9.14 us -> none  [the longest x1 5.87 us: in_one_piece(): done.append(lax.slice_in_dim(out, at, at + a.shape[along], axis=along))]
    dot_general x2 -> x0, matrix products: 8.26 us -> none  [the longest x1 5.24 us: local(): jnp.einsum('irc,nc->rin', qkv_grads, qkv_weight, preferred_element_type=j...]
  transfers between devices with their start and end apart: 3 -> 1, of which waited for: 2 -> 0; matrix products, arithmetic and copies ran while one was open for 18% -> 0% of each run, Pallas kernels for 0% -> 58%
where the time goes in v2:
time: 144 us; the launch traced here: 145 us
  Pallas kernels  127 us (88%)
  starting transfers between devices  8.12 us (6%)
  local copies, waits for them, and re-layouts  7.25 us (5%)
  other arithmetic  2.06 us (1%)
    pallas_call x1, Pallas kernels, back(): pl.pallas_call(back_kernel, name='back', out_shape=(jax.ShapeDtypeStruct(...  74.3 us
    pallas_call x1, Pallas kernels, front(): pl.pallas_call(front_kernel, name='front', out_shape=(jax.ShapeDtypeStruc...  42.9 us
    pallas_call x1, Pallas kernels, attend(): pl.pallas_call(attn_kernel, name='attend', out_shape=(jax.ShapeDtypeStruc...  9.3 us
    all_to_all x1, starting transfers between devices, local(): lax.all_to_all(part, 'wide', split_axis=0, concat_axis=0, tiled=True)  8.12 us
    unnamed x24, local copies, waits for them, and re-layouts  7.25 us
  transfers between devices with their start and end apart: 1, of which 0 were waited for; matrix products, arithmetic and copies ran while one was open for 0% of the time, Pallas kernels for 58%

profile of v2, /device:TPU:23, one launch (start us, length us, event | category | flops | bytes accessed | tf_op | source)
XLA Modules:
  0.0 144.7 jit_solution(13053980351278580849)
XLA Ops:
  0.6 0.0 copy-start
  0.6 1.6 %copy-done = bf16[256,4096]{1,0:T(8,128)(2,1)S(1)} copy-done((bf16[256,4096]{1,0:T(8,128)(2,1)S(1)}, bf16[256,4096]{1,0:T(8,128)(2,1)}, u32[]{:S(2)}) %copy-start) | copy-done | bytes 2097176
  2.2 1.2 copy-done.2
  3.5 1.2 copy-done.3
  4.7 0.9 copy-done.5
  5.6 0.9 copy-done.7
  6.5 42.9 %front.1 = (bf16[256,256]{1,0:T(8,128)(2,1)S(1)}, bf16[2,8,512,128]{3,2,1,0:T(8,128)(2,1)S(1)}, bf16[8,256,256]{2,1,0:T(8,128)(2,1)}) custom-call(bf16[512,128]{1,0:T(8,128)(2,1)S(1)} %copy-done.7, bf16[256,4096]{1,0:T(8,128)(2,1)S(1)} %copy-done, bf16[512,1024]{1,0:T(8,128)(2,1)S(1)} %copy-done.2, bf16[512,1024]{1,0:T(8,128)(2,1)S(1)} %copy-done.3, ...), custom_call_target="tpu_custom_call" | custom-call | flops 2000000000 | bytes 20000000 | tf_op jit(solution)/shard_map/front/pallas_call | solution.py:169
  49.5 0.0 copy-start.4
  49.5 0.0 copy-start.6
  49.5 0.0 copy-start.9
  49.5 0.0 copy-start.10
  49.5 8.1 %all-to-all-start = ((bf16[8,256,256]{2,1,0:T(8,128)(2,1)}), bf16[8,256,256]{2,1,0:T(8,128)(2,1)}, u32[]{:S(2)}, u32[]{:S(2)}) async-start(bf16[8,256,256]{2,1,0:T(8,128)(2,1)} %get-tuple-element.15), calls=%async_computation | async-start | bytes 2097152 | tf_op jit(solution)/shard_map/all_to_all | solution.py:573
  57.6 0.0 copy-done.4
  57.6 0.0 copy-done.6
  57.6 0.0 copy-done.9
  57.6 0.0 copy-done.10
  57.6 0.0 copy-start.1
  57.7 0.0 copy-start.8
  57.7 9.3 %attend.1 = (bf16[256,256]{1,0:T(8,128)(2,1)S(1)}, bf16[8,2,256,256]{3,2,1,0:T(8,128)(2,1)S(1)}) custom-call(s32[4096]{0:T(1024)S(1)} %copy-done.10, bf16[512,256]{1,0:T(8,128)(2,1)S(1)} %copy-done.4, bf16[256,256]{1,0:T(8,128)(2,1)S(1)} %get-tuple-element.10.ag, bf16[512,256]{1,0:T(8,128)(2,1)S(1)} %copy-done.6, f32[2,4096]{1,0:T(2,128)S(1)} %copy-done.9, ...), custom_call_target="tpu_custom_call" | custom-call | flops 5000000000 | bytes 6000000 | tf_op jit(solution)/shard_map/attend/pallas_call | solution.py:260
  67.0 74.3 %back.1 = (bf16[512,128]{1,0:T(8,128)(2,1)S(1)}, bf16[128,768]{1,0:T(8,128)(2,1)S(1)}) custom-call(bf16[256,256]{1,0:T(8,128)(2,1)S(1)} %get-tuple-element.12.dq, bf16[8,2,256,256]{3,2,1,0:T(8,128)(2,1)S(1)} %get-tuple-element.13.dkv, bf16[512,128]{1,0:T(8,128)(2,1)S(1)} %copy-done.8, bf16[128,6144]{1,0:T(8,128)(2,1)S(1)} %copy-done.1), custom_call_target="tpu_custom_call" | custom-call | flops 3000000000 | bytes 20000000 | tf_op jit(solution)/shard_map/back/pallas_call | solution.py:538
  141.3 0.0 all-to-all-done
  141.3 2.1 %reduce_sum.12 = bf16[256,256]{1,0:T(8,128)(2,1)} reduce(bf16[8,256,256]{2,1,0:T(8,128)(2,1)} %all-to-all-done, bf16[]{:T(256)} %constant.2.clone.1), dimensions={0}, to_apply=%region_0.0 | reduce | flops 458752 | bytes 1179650 | tf_op jit(solution)/shard_map/reduce_sum | solution.py:578
  143.4 0.7 copy.15
  144.0 0.7 copy.16
  (6 shorter events, 0.0 us)
Async XLA Ops:
  0.6 1.6 %copy-start = (bf16[256,4096]{1,0:T(8,128)(2,1)S(1)}, bf16[256,4096]{1,0:T(8,128)(2,1)}, u32[]{:S(2)}) copy-start(bf16[256,4096]{1,0:T(8,128)(2,1)} %ow.1) | copy-start | bytes 6291460
  2.2 1.2 copy-start.2
  3.4 1.2 copy-start.3
  4.7 0.9 copy-start.5
  5.6 0.9 copy-start.7
  49.5 8.2 %copy-start.4 = (bf16[512,256]{1,0:T(8,128)(2,1)S(1)}, bf16[512,256]{1,0:T(8,128)(2,1)}, u32[]{:S(2)}) copy-start(bf16[512,256]{1,0:T(8,128)(2,1)} %q_ref.1) | copy-start | bytes 786436
  49.5 8.2 %copy-start.6 = (bf16[512,256]{1,0:T(8,128)(2,1)S(1)}, bf16[512,256]{1,0:T(8,128)(2,1)}, u32[]{:S(2)}) copy-start(bf16[512,256]{1,0:T(8,128)(2,1)} %ao.3) | copy-start | bytes 786436
  49.5 8.2 %copy-start.9 = (f32[2,4096]{1,0:T(2,128)S(1)}, f32[2,4096]{1,0:T(2,128)}, u32[]{:S(2)}) copy-start(f32[2,4096]{1,0:T(2,128)} %lse.1) | copy-start | bytes 98308
  49.5 8.1 %copy-start.10 = (s32[4096]{0:T(1024)S(1)}, s32[4096]{0:T(1024)}, u32[]{:S(2)}) copy-start(s32[4096]{0:T(1024)} %docs.1) | copy-start | bytes 49156
  49.5 91.8 %all-to-all-start = ((bf16[8,256,256]{2,1,0:T(8,128)(2,1)}), bf16[8,256,256]{2,1,0:T(8,128)(2,1)}, u32[]{:S(2)}, u32[]{:S(2)}) async-start(bf16[8,256,256]{2,1,0:T(8,128)(2,1)} %get-tuple-element.15), calls=%async_computation | async-start | bytes 2097152 | tf_op jit(solution)/shard_map/all_to_all | solution.py:573
  57.6 9.3 %copy-start.1 = (bf16[128,6144]{1,0:T(8,128)(2,1)S(1)}, bf16[128,6144]{1,0:T(8,128)(2,1)}, u32[]{:S(2)}) copy-start(bf16[128,6144]{1,0:T(8,128)(2,1)} %wq.1) | copy-start | bytes 4718596
  57.7 9.3 %copy-start.8 = (bf16[512,128]{1,0:T(8,128)(2,1)S(1)}, bf16[512,128]{1,0:T(8,128)(2,1)}, u32[]{:S(2)}) copy-start(bf16[512,128]{1,0:T(8,128)(2,1)} %normed.1) | copy-start | bytes 393220

commit v3 on v1

v3 whole, which is shorter than its diff:
```python
import jax
import jax.numpy as jnp
from jax import lax
from jax.experimental import pallas as pl
from jax.experimental.pallas import tpu as pltpu
from jax.sharding import PartitionSpec as P

MESH = pl.DeviceIdType.MESH
D = 4096
HEAD_SIZE = 128
QB = 256
LOG2E = 1.4426950408889634
SCALE = HEAD_SIZE ** (-0.5)
NT = (((1,), (1,)), ((), ()))
TN = (((0,), (0,)), ((), ()))
NN = (((1,), (0,)), ((), ()))


def dot(a, b, dims):
    return lax.dot_general(a, b, dims, preferred_element_type=jnp.float32)


def aligned(at, size):
    return pl.ds(pl.multiple_of(at * size, size), size)


def remote(src, dst, send, recv, where):
    return pltpu.make_async_remote_copy(
        src_ref=src, dst_ref=dst, send_sem=send, recv_sem=recv, device_id=where, device_id_type=MESH
    )


def greet(places):
    barrier = pltpu.get_barrier_semaphore()
    for where in places:
        pl.semaphore_signal(barrier, inc=1, device_id=where, device_id_type=MESH)
    pl.semaphore_wait(barrier, len(places))


def place():
    r = lax.axis_index("role")
    w = lax.axis_index("wide")
    t = lax.axis_index("tp")
    return r, w, t, t // 2, t % 2


def plane_peer(w, z, xl, k):
    dx, dy = k // 4, k % 4
    peer = ((w // 4 + dx) % 2) * 4 + (w % 4 + dy) % 4
    return {"wide": peer, "tp": z * 2 + (xl if dx == 0 else 1 - xl)}


class Gather:
    def __init__(self, block, zs, zr, xs, xr):
        self.block, self.zs, self.zr, self.xs, self.xr = block, zs, zr, xs, xr
        r, w, t, self.z, self.xl = place()
        self.ways = (
            {"tp": ((self.z + 1) % 8) * 2 + self.xl},
            {"tp": ((self.z + 7) % 8) * 2 + self.xl},
        )
        self.inner = {"tp": self.z * 2 + 1 - self.xl}
        self.sent, self.hops, self.crossed = [], {}, {}

    def at(self, d, s):
        return (self.z + 8 - s) % 8 if d == 0 else (self.z + s) % 8

    def piece(self, at, j, share=None):
        if j < 2:
            return self.block(at, self.xl, 128 * j, 128)
        if share is None:
            return self.block(at, 1 - self.xl, 0, 128)
        return self.block(at, 1 - self.xl, 64 * share, 64)

    def go(self, ref, send, recv, where):
        c = remote(ref, ref, send, recv, where)
        c.start()
        self.sent.append(c)
        return c

    def hop(self, d, s, j):
        ref = self.piece(self.at(d, s), j, d if s == 3 else None)
        self.hops[d, s, j] = self.go(ref, self.zs.at[d, s, j], self.zr.at[d, s, j], self.ways[d])

    def cross(self, at, j, k):
        self.crossed[k] = self.go(self.piece(at, j), self.xs.at[k], self.xr.at[k], self.inner)

    def start(self):
        for j in range(2):
            self.hop(0, 0, j)
            self.hop(1, 0, j)
            self.cross(self.z, j, 8 if j == 0 else 0)

    def second(self):
        self.crossed[8].wait_recv()
        self.hop(0, 0, 2)
        self.hop(1, 0, 2)

    def step(self, s, j):
        for d in range(2):
            if s == 4 and j < 2 and d != j:
                continue
            self.hops[d, s - 1, j].wait_recv()
            if s < 3 or (s == 3 and (j == 2 or d == j)):
                self.hop(d, s, j)
            if j == 1:
                self.cross(self.at(d, s), 1, 7 if s == 4 else 2 * s - 1 + d)

    def whole(self, s):
        for k in ((0,), (1, 2), (3, 4), (5, 6), (7,))[s]:
            self.crossed[k].wait_recv()

    def blocks(self, s):
        return ((self.z + 8 - s) % 8, (self.z + s) % 8) if s in (1, 2, 3) else ((self.z + s) % 8,)

    def finish(self):
        for c in self.sent:
            c.wait_send()


def count_below(docs, value):
    below = jnp.where(docs < value, 1.0, 0.0)
    count = jnp.sum(jnp.sum(below, axis=0, keepdims=True), axis=1, keepdims=True)
    return count.astype(jnp.int32)


def whole_kernel(
    normed, queries, keys, values, ao, lse_in, og, ow, wq_in, docs_in,
    ng_out, ow_out, gw_out,
    docs, G, O, W, AO, OP, OR, acc, kv, Q, lse, q2, g2, dq, dqb, dkv,
    QF, KF, D1, S, D2, F, FR, N, wq, nacc, kacc,
    lsem, swap_sem, k_send, k_recv, kp_sem, ao_sem, aoh_sem, n_sem, o_send, o_recv,
    az_s, az_r, ax_s, ax_r, ah_s, ah_r,
    ez_s, ez_r, ex_s, ex_r, eh_s, eh_r,
    vz_s, vz_r, vx_s, vx_r, vh_s, vh_r,
    d1s, d1r, d2s, d2r, f_send, f_recv,
):
    r, w, t, z, xl = place()
    low = jnp.bfloat16
    partner = {"role": 1 - r}
    inner = {"tp": z * 2 + 1 - xl}
    up = {"tp": ((z + 1) % 8) * 2 + xl}
    down = {"tp": ((z + 7) % 8) * 2 + xl}
    plane = [{"wide": (w + k // 2) % 8, "tp": z * 2 + (xl + k % 2) % 2} for k in range(1, 16)]
    cols = aligned(xl, 128)
    mine = aligned(r, QB)
    other = aligned(1 - r, QB)
    heads = aligned(z, 128)

    @pl.when(r == 0)
    def _():
        pltpu.make_async_copy(keys.at[:, heads], kv.at[r, w], lsem.at[0]).start()

    @pl.when(r == 1)
    def _():
        pltpu.make_async_copy(values.at[:, heads], kv.at[r, w], lsem.at[0]).start()

    load_own = pltpu.make_async_copy(og.at[mine, :], G.at[z, r, :, cols], lsem.at[1])
    load_ao = pltpu.make_async_copy(ao, AO.at[0], lsem.at[2])
    load_w = pltpu.make_async_copy(ow, W, lsem.at[3])
    load_docs = pltpu.make_async_copy(docs_in, docs, lsem.at[4])
    load_q = pltpu.make_async_copy(queries.at[mine, :], Q, lsem.at[5])
    load_lse = pltpu.make_async_copy(lse_in, lse, lsem.at[6])
    load_n = pltpu.make_async_copy(normed, N.at[0], lsem.at[7])
    load_wq = pltpu.make_async_copy(wq_in, wq, lsem.at[8])
    for c in (load_own, load_ao, load_w, load_docs, load_q, load_lse, load_n, load_wq):
        c.start()

    greet([partner, up, down] + plane)

    swap = remote(
        og.at[other, :], G.at[z, r, :, cols], swap_sem.at[0], swap_sem.at[1], partner
    )
    swap.start()
    sends = [swap]
    load_ao.wait()
    lend = remote(AO.at[0, mine], AO.at[1, mine], ao_sem.at[0], ao_sem.at[1], inner)
    lend.start()
    sends.append(lend)
    pltpu.make_async_copy(keys.at[:, heads], kv.at[r, w], lsem.at[0]).wait()
    pushes = []
    for k in range(1, 8):
        c = remote(
            kv.at[r, w], kv.at[r, w], k_send.at[k - 1], k_recv.at[k - 1], plane_peer(w, z, xl, k)
        )
        c.start()
        pushes.append(c)
    load_own.wait()
    swap.wait_recv()

    A = Gather(
        lambda at, x, row, n: G.at[at, :, pl.ds(row, n), aligned(x, 128)], az_s, az_r, ax_s, ax_r
    )
    A.start()
    load_w.wait()
    acc[...] = jnp.zeros_like(acc)
    A.second()

    order, hands = [], []

    def give(at):
        k = len(order)
        c = remote(G.at[at, 1 - r], O.at[at], ah_s.at[k], ah_r.at[k], partner)
        c.start()
        order.append(at)
        hands.append(c)

    def use(at):
        low_cols = aligned(at, QB)
        high_cols = aligned(at + 8, QB)
        acc[...] += dot(G[at, 0], W[:, low_cols], NT) + dot(G[at, 1], W[:, high_cols], NT)

    def out_chunk(at):
        far = (at // 4 + w // 4) % 2
        return remote(
            OP.at[at], OR.at[w], o_send.at[at], o_recv.at[w],
            {"wide": at, "tp": z * 2 + (xl + far) % 2},
        )

    def product(k):
        at = order[k]
        far = (at // 4 + w // 4) % 2
        hands[k].wait_recv()
        total = dot(AO[far, mine, :], G[at, r], TN) + dot(AO[far, other, :], O[at], TN)
        OP[at] = total.astype(low)

        @pl.when(at != w)
        def _():
            out_chunk(at).start()

    def whole(s):
        A.whole(s)
        for at in A.blocks(s):
            give(at)

    A.step(1, 0)
    A.step(1, 1)
    lend.wait_recv()
    lent = remote(AO.at[1, mine], AO.at[1, mine], aoh_sem.at[0], aoh_sem.at[1], partner)
    lent.start()
    sends.append(lent)
    A.step(1, 2)
    whole(0)
    lent.wait_recv()
    A.step(2, 0)
    A.step(2, 1)
    use(order[0])
    product(0)
    A.step(2, 2)
    whole(1)
    A.step(3, 0)
    use(order[1])
    A.step(3, 1)
    use(order[2])
    product(1)
    A.step(3, 2)
    product(2)
    whole(2)
    A.step(4, 0)
    use(order[3])
    product(3)
    A.step(4, 1)
    use(order[4])
    product(4)
    for c in pushes:
        c.wait_recv()
    hand_kv = remote(kv.at[r], kv.at[r], kp_sem.at[0], kp_sem.at[1], partner)
    hand_kv.start()
    sends.append(hand_kv)
    A.step(4, 2)
    whole(3)
    use(order[5])
    use(order[6])
    whole(4)
    use(order[7])

    load_n.wait()
    lend_n = remote(N.at[0], N.at[1], n_sem.at[0], n_sem.at[1], inner)
    lend_n.start()
    sends.append(lend_n)
    load_docs.wait()
    load_q.wait()
    load_lse.wait()
    start_at = (2 * w + r) * QB
    c1 = count_below(docs[...], 1)
    c2 = count_below(docs[...], 2)
    span = aligned(2 * w + r, QB)
    deltas, lses = [], []
    for h in range(2):
        hc = pl.ds(h * 128, 128)
        q2[pl.ds(h * QB, QB), :] = Q[:, hc]
        g = acc[:, hc].astype(low)
        g2[pl.ds(h * QB, QB), :] = g
        both = g.astype(jnp.float32) * AO[0, mine, hc].astype(jnp.float32)
        deltas.append(jnp.sum(both.T, axis=0, keepdims=True))
        lses.append(lse[pl.ds(h, 1), span] * LOG2E)
    delta = jnp.concatenate(deltas, axis=1)
    lse2 = jnp.concatenate(lses, axis=1)
    lane = lax.broadcasted_iota(jnp.int32, (1, 2 * QB), 1)
    q_pos = start_at + jnp.where(lane >= QB, lane - QB, lane)
    q_start = jnp.where(q_pos >= c2, c2, jnp.where(q_pos >= c1, c1, 0))
    dq[...] = jnp.zeros_like(dq)
    product(5)
    product(6)
    product(7)
    hand_kv.wait_recv()

    def first(wp):
        return remote(dkv.at[wp, 1 - r], D1.at[wp], d1s.at[wp], d1r.at[wp], partner)

    def second(wp, kind):
        return remote(
            S.at[wp, kind], D2.at[w, xl], d2s.at[wp, kind], d2r.at[w, xl],
            {"wide": wp, "tp": z * 2 + kind},
        )

    def arrive(ws, xs):
        return remote(
            S.at[w, xl], D2.at[ws, xs], d2s.at[w, xl], d2r.at[ws, xs],
            {"wide": ws, "tp": z * 2 + xs},
        )

    def pair_sum(wp):
        first(wp).wait_recv()
        both = (dkv[wp, r].astype(jnp.float32) + D1[wp].astype(jnp.float32)).astype(low)
        S[wp, 0] = both[:, 0:128]
        S[wp, 1] = both[:, 128:256]

    @pl.loop(0, w + 1)
    def _(i):
        k_rows = kv[0, i]
        v_rows = kv[1, i]
        scores = dot(k_rows, q2[...], NT)
        k_pos = i * 512 + lax.broadcasted_iota(jnp.int32, (512, 1), 0)
        allowed = (k_pos <= q_pos) & (k_pos >= q_start)
        probs = jnp.where(allowed, jnp.exp2(scores * (SCALE * LOG2E) - lse2), 0.0)
        dv = dot(probs.astype(low), g2[...], NN).astype(low)
        prob_grad = dot(v_rows, g2[...], NT)
        ds = (probs * (prob_grad - delta)).astype(low)
        dk = (dot(ds, q2[...], NN) * SCALE).astype(low)
        dq[...] += dot(ds, k_rows, TN)
        for h in range(2):
            dkv[i, h, :, 0:128] = dk[h * QB:(h + 1) * QB, :]
            dkv[i, h, :, 128:256] = dv[h * QB:(h + 1) * QB, :]
        first(i).start()

        @pl.when(i > 0)
        def _():
            pair_sum(i - 1)
            second(i - 1, 0).start()
            second(i - 1, 1).start()

    for h in range(2):
        dqb[:, h * 128:(h + 1) * 128] = (dq[pl.ds(h * QB, QB), :] * SCALE).astype(low)
    QF[r, z, xl] = dqb[...]
    pair_sum(w)
    second(w, 1 - xl).start()

    E = Gather(lambda at, x, row, n: QF.at[r, at, x, pl.ds(row, n), :], ez_s, ez_r, ex_s, ex_r)
    V = Gather(lambda at, x, row, n: KF.at[r, at, x, pl.ds(row, n), :], vz_s, vz_r, vx_s, vx_r)
    E.start()
    load_wq.wait()
    nacc[...] = jnp.zeros_like(nacc)

    E.second()

    def key_sums():
        kacc[...] = S[w, xl].astype(jnp.float32)

        @pl.loop(w + 1, 8)
        def _(ws):
            for xs in range(2):
                arrive(ws, xs).wait_recv()
                kacc[...] += D2[ws, xs].astype(jnp.float32)

        arrive(w, 1 - xl).wait_recv()
        KF[r, z, xl] = (kacc[...] + D2[w, 1 - xl].astype(jnp.float32)).astype(low)

    e_order, e_hands, v_order, v_hands = [], [], [], []

    def pass_on(gather, s, buf, ss, rs, seen, copies):
        gather.whole(s)
        for at in gather.blocks(s):
            k = len(seen)
            c = remote(buf.at[r, at], buf.at[r, at], ss.at[k], rs.at[k], partner)
            c.start()
            seen.append(at)
            copies.append(c)

    def e_whole(s):
        pass_on(E, s, QF, eh_s, eh_r, e_order, e_hands)

    def v_whole(s):
        pass_on(V, s, KF, vh_s, vh_r, v_order, v_hands)

    def process(k):
        at = e_order[k]
        e_hands[k].wait_recv()
        for x in range(2):
            weight = wq[:, aligned(2 * at + x, QB)]
            far = (((2 * at + x) // 3) // 4 + w // 4) % 2
            for h in range(2):
                nacc[h] += dot(QF[h, at, x], weight, NT)
            total = dot(N[far, 0:QB, :], QF[0, at, x], TN) + dot(N[far, QB:512, :], QF[1, at, x], TN)
            F[4 * at + 2 * x] = total[:, 0:128].astype(low)
            F[4 * at + 2 * x + 1] = total[:, 128:256].astype(low)

            @pl.when((2 * at + x) // 3 != w)
            def _():
                two(2 * at + x).start()

    def process_kv(k):
        at = v_order[k]
        v_hands[k].wait_recv()
        for x in range(2):
            spot = 32 + 8 * x + at
            weight = wq[:, aligned(spot, 128)]
            far = ((spot // 6) // 4 + w // 4) % 2
            for h in range(2):
                nacc[h] += dot(KF[h, at, x], weight, NT)
            total = dot(N[far, 0:QB, :], KF[0, at, x], TN) + dot(N[far, QB:512, :], KF[1, at, x], TN)
            F[spot] = total.astype(low)

            @pl.when(spot // 6 != w)
            def _():
                one(spot).start()

    def peer(wp):
        far = (wp // 4 + w // 4) % 2
        return {"wide": wp, "tp": z * 2 + (xl + far) % 2}

    def two(tp):
        return remote(
            F.at[pl.ds(2 * tp, 2)], FR.at[w, pl.ds(2 * (tp % 3), 2)],
            f_send.at[2 * tp], f_recv.at[w, 2 * (tp % 3)], peer(tp // 3),
        )

    def one(spot):
        return remote(
            F.at[spot], FR.at[w, spot % 6], f_send.at[spot], f_recv.at[w, spot % 6], peer(spot // 6)
        )

    def two_in(ws, j):
        return remote(
            F.at[pl.ds(6 * w + 2 * j, 2)], FR.at[ws, pl.ds(2 * j, 2)],
            f_send.at[6 * w + 2 * j], f_recv.at[ws, 2 * j], peer(ws),
        )

    def one_in(ws, j):
        return remote(F.at[6 * w + j], FR.at[ws, j], f_send.at[6 * w + j], f_recv.at[ws, j], peer(ws))

    E.step(1, 0)
    lend_n.wait_recv()
    E.step(1, 1)
    key_sums()
    V.start()
    E.step(1, 2)
    V.second()
    e_whole(0)
    E.step(2, 0)
    E.step(2, 1)
    V.step(1, 0)
    V.step(1, 1)
    process(0)
    E.step(2, 2)
    V.step(1, 2)
    e_whole(1)
    v_whole(0)
    E.step(3, 0)
    process(1)
    E.step(3, 1)
    V.step(2, 0)
    V.step(2, 1)
    process(2)
    E.step(3, 2)
    V.step(2, 2)
    process_kv(0)
    e_whole(2)
    v_whole(1)
    E.step(4, 0)
    process(3)
    E.step(4, 1)
    V.step(3, 0)
    V.step(3, 1)
    process(4)
    E.step(4, 2)
    V.step(3, 2)
    process_kv(1)
    process_kv(2)
    e_whole(3)
    v_whole(2)
    process(5)
    process(6)
    e_whole(4)
    V.step(4, 0)
    V.step(4, 1)
    V.step(4, 2)
    process_kv(3)
    process_kv(4)
    process(7)
    v_whole(3)
    v_whole(4)
    process_kv(5)
    process_kv(6)
    process_kv(7)

    for h in range(2):
        ng_out[h * QB:(h + 1) * QB, :] = nacc[h].astype(low)

    OR[w] = OP[w]

    @pl.loop(0, 8)
    def _(ws):
        @pl.when(ws != w)
        def _():
            far = (ws // 4 + w // 4) % 2
            remote(
                OP.at[w], OR.at[ws], o_send.at[w], o_recv.at[ws],
                {"wide": ws, "tp": z * 2 + (xl + far) % 2},
            ).wait_recv()

    total = OR[0].astype(jnp.float32)
    for ws in range(1, 8):
        total += OR[ws].astype(jnp.float32)
    ow_out[...] = total.astype(low)

    FR[w] = F[pl.ds(6 * w, 6)]

    @pl.loop(0, 8)
    def _(ws):
        @pl.when(ws != w)
        def _():
            for j in range(3):
                @pl.when((w < 5) | ((w == 5) & (j == 0)))
                def _():
                    two_in(ws, j).wait_recv()

            for j in range(6):
                @pl.when((w > 5) | ((w == 5) & (j > 1)))
                def _():
                    one_in(ws, j).wait_recv()

    for j in range(6):
        total = FR[0, j].astype(jnp.float32)
        for ws in range(1, 8):
            total += FR[ws, j].astype(jnp.float32)
        gw_out[:, j * 128:(j + 1) * 128] = total.astype(low)

    for c in sends + pushes + hands + e_hands + v_hands:
        c.wait_send()
    for gather in (A, E, V):
        gather.finish()

    @pl.loop(0, w)
    def _(wp):
        first(wp).wait_send()
        second(wp, 0).wait_send()
        second(wp, 1).wait_send()

    first(w).wait_send()
    second(w, 1 - xl).wait_send()

    @pl.loop(0, 8)
    def _(wp):
        @pl.when(wp != w)
        def _():
            out_chunk(wp).wait_send()

    @pl.loop(0, 16)
    def _(tp):
        @pl.when(tp // 3 != w)
        def _():
            two(tp).wait_send()

        @pl.when((32 + tp) // 6 != w)
        def _():
            one(32 + tp).wait_send()


def local(
    normed, queries, keys, values, attn_out, row_logsumexp, out_grad, out_weight, qkv_weight, documents, tasks
):
    hbm = pl.BlockSpec(memory_space=pltpu.HBM)
    vmem = pl.BlockSpec(memory_space=pltpu.VMEM)
    dma = pltpu.SemaphoreType.DMA
    low, wide = jnp.bfloat16, jnp.float32
    ring = [dma((2, 4, 3)), dma((2, 4, 3)), dma((9,)), dma((9,)), dma((8,)), dma((8,))]
    return pl.pallas_call(
        whole_kernel,
        name="layer",
        out_shape=(
            jax.ShapeDtypeStruct((512, 128), low),
            jax.ShapeDtypeStruct((QB, QB), low),
            jax.ShapeDtypeStruct((128, 768), low),
        ),
        in_specs=[hbm] * 10,
        out_specs=(vmem, vmem, vmem),
        scratch_shapes=[
            pltpu.VMEM((32, 128), jnp.int32),
            pltpu.VMEM((8, 2, QB, QB), low),
            pltpu.VMEM((8, QB, QB), low),
            pltpu.VMEM((QB, D), low),
            pltpu.VMEM((2, 512, QB), low),
            pltpu.VMEM((8, QB, QB), low),
            pltpu.VMEM((8, QB, QB), low),
            pltpu.VMEM((QB, QB), wide),
            pltpu.VMEM((2, 8, 512, 128), low),
            pltpu.VMEM((QB, QB), low),
            pltpu.VMEM((2, 4096), wide),
            pltpu.VMEM((512, 128), low),
            pltpu.VMEM((512, 128), low),
            pltpu.VMEM((512, 128), wide),
            pltpu.VMEM((QB, QB), low),
            pltpu.VMEM((8, 2, QB, QB), low),
            pltpu.VMEM((2, 8, 2, QB, QB), low),
            pltpu.VMEM((2, 8, 2, QB, 128), low),
            pltpu.VMEM((8, QB, QB), low),
            pltpu.VMEM((8, 2, QB, 128), low),
            pltpu.VMEM((8, 2, QB, 128), low),
            pltpu.VMEM((48, 128, 128), low),
            pltpu.VMEM((8, 6, 128, 128), low),
            pltpu.VMEM((2, 512, 128), low),
            pltpu.VMEM((128, 6144), low),
            pltpu.VMEM((2, QB, 128), wide),
            pltpu.VMEM((QB, 128), wide),
            dma((9,)), dma((2,)), dma((7,)), dma((7,)), dma((2,)), dma((2,)), dma((2,)), dma((2,)),
            dma((8,)), dma((8,)),
        ]
        + ring * 3
        + [dma((8,)), dma((8,)), dma((8, 2)), dma((8, 2)), dma((48,)), dma((8, 6))],
        compiler_params=pltpu.CompilerParams(
            collective_id=0, has_side_effects=True, vmem_limit_bytes=60 * 1024 * 1024
        ),
        cost_estimate=pl.CostEstimate(
            flops=10_000_000_000, bytes_accessed=40_000_000, transcendentals=2_000_000
        ),
    )(
        normed, queries, keys, values, attn_out, row_logsumexp, out_grad, out_weight, qkv_weight,
        documents.reshape(32, 128),
    )


def solution(mesh):
    in_specs = (
        P("wide", ("role", "tp")),
        P("wide", "tp"),
        P("wide", None),
        P("wide", None),
        P("wide", "tp"),
        P("tp", None),
        P("wide", ("role", "tp")),
        P("tp", None),
        P(("role", "tp"), None),
        P(),
        P(),
    )
    out_specs = (P("wide", ("role", "tp")), P("tp", ("role", "wide")), P(("role", "tp"), "wide"))
    return jax.shard_map(local, mesh=mesh, in_specs=in_specs, out_specs=out_specs, check_vma=False)
```

time: 269 us -> 105 us (0.39)
  the two profiles are of different devices: /device:TPU:23 before, /device:TPU:17 now
where the time goes in v3:
time: 105 us
  Pallas kernels  99.3 us (95%)
  local copies, waits for them, and re-layouts  4.75 us (5%)
    pallas_call x1, Pallas kernels, local(): pl.pallas_call(whole_kernel, name='layer', out_shape=(jax.ShapeDtypeStruc...  99.3 us
    unnamed x3, local copies, waits for them, and re-layouts  4.75 us

profile of v3, /device:TPU:17, one launch (start us, length us, event | category | flops | bytes accessed | tf_op | source)
XLA Modules:
  0.0 104.7 jit_solution(16099976484001133155)
XLA Ops:
  0.6 99.3 %layer.1 = (bf16[512,128]{1,0:T(8,128)(2,1)}, bf16[256,256]{1,0:T(8,128)(2,1)}, bf16[128,768]{1,0:T(8,128)(2,1)}) custom-call(bf16[512,128]{1,0:T(8,128)(2,1)} %normed.1, bf16[512,256]{1,0:T(8,128)(2,1)} %queries.1, bf16[512,1024]{1,0:T(8,128)(2,1)} %keys.1, bf16[512,1024]{1,0:T(8,128)(2,1)} %values.1, bf16[512,256]{1,0:T(8,128)(2,1)} %ao.1, ...), custom_call_target="tpu_custom_call" | custom-call | flops 10000000000 | bytes 40000000 | tf_op jit(solution)/shard_map/layer/pallas_call | solution.py:587
  100.0 1.6 %copy.16 = bf16[512,128]{1,0:T(8,128)(2,1)} copy(bf16[512,128]{1,0:T(8,128)(2,1)} %get-tuple-element.6) | data formatting | bytes 262144
  101.5 1.6 %copy.17 = bf16[256,256]{1,0:T(8,128)(2,1)} copy(bf16[256,256]{1,0:T(8,128)(2,1)} %get-tuple-element.7) | data formatting | bytes 262144
  103.1 1.6 %copy.18 = bf16[128,768]{1,0:T(8,128)(2,1)} copy(bf16[128,768]{1,0:T(8,128)(2,1)} %get-tuple-element.8) | data formatting | bytes 393216

commit v4 on v3

--- a/solution.py
+++ b/solution.py
@@ -126,18 +126,20 @@
 def whole_kernel(
     normed, queries, keys, values, ao, lse_in, og, ow, wq_in, docs_in,
     ng_out, ow_out, gw_out,
-    docs, G, O, W, AO, OP, OR, acc, kv, Q, lse, q2, g2, dq, dqb, dkv,
-    QF, KF, D1, S, D2, F, FR, N, wq, nacc, kacc,
-    lsem, swap_sem, k_send, k_recv, kp_sem, ao_sem, aoh_sem, n_sem, o_send, o_recv,
+    docs, G, O, W, AO, OP, OX, OR, acc, kv, Q, lse, q2, g2, dq, dqb, dkv,
+    QF, KF, D1, S, D2, F, FX, FR, N, wq, nacc, kacc,
+    lsem, swap_sem, k_send, k_recv, kp_sem, ao_sem, aoh_sem, n_sem, o_send, ox_recv, o_recv,
     az_s, az_r, ax_s, ax_r, ah_s, ah_r,
     ez_s, ez_r, ex_s, ex_r, eh_s, eh_r,
     vz_s, vz_r, vx_s, vx_r, vh_s, vh_r,
-    d1s, d1r, d2s, d2r, f_send, f_recv,
+    d1s, d1r, d2s, d2r, f_send, fx_recv, f_recv,
 ):
     r, w, t, z, xl = place()
     low = jnp.bfloat16
     partner = {"role": 1 - r}
     inner = {"tp": z * 2 + 1 - xl}
+    outer = {"wide": (w + 4) % 8, "tp": z * 2 + 1 - xl}
+    side = w % 4
     up = {"tp": ((z + 1) % 8) * 2 + xl}
     down = {"tp": ((z + 7) % 8) * 2 + xl}
     plane = [{"wide": (w + k // 2) % 8, "tp": z * 2 + (xl + k % 2) % 2} for k in range(1, 16)]
@@ -209,21 +211,35 @@
         high_cols = aligned(at + 8, QB)
         acc[...] += dot(G[at, 0], W[:, low_cols], NT) + dot(G[at, 1], W[:, high_cols], NT)
 
+    def across(wp):
+        return (wp // 4 + w // 4) % 2
+
+    def out_cross(at):
+        return remote(OP.at[at], OX.at[at], o_send.at[at], ox_recv.at[at], outer)
+
     def out_chunk(at):
-        far = (at // 4 + w // 4) % 2
-        return remote(
-            OP.at[at], OR.at[w], o_send.at[at], o_recv.at[w],
-            {"wide": at, "tp": z * 2 + (xl + far) % 2},
-        )
+        return remote(OP.at[at], OR.at[side], o_send.at[at], o_recv.at[side], {"wide": at})
 
     def product(k):
         at = order[k]
-        far = (at // 4 + w // 4) % 2
+        far = across(at)
         hands[k].wait_recv()
         total = dot(AO[far, mine, :], G[at, r], TN) + dot(AO[far, other, :], O[at], TN)
         OP[at] = total.astype(low)
 
-        @pl.when(at != w)
+        @pl.when(far == 1)
+        def _():
+            out_cross(at).start()
+
+    def out_merge(k):
+        at = order[k]
+
+        @pl.when(across(at) == 0)
+        def _():
+            out_cross(at).wait_recv()
+            OP[at] = (OP[at].astype(jnp.float32) + OX[at].astype(jnp.float32)).astype(low)
+
+        @pl.when((across(at) == 0) & (at != w))
         def _():
             out_chunk(at).start()
 
@@ -254,6 +270,7 @@
     product(1)
     A.step(3, 2)
     product(2)
+    out_merge(0)
     whole(2)
     A.step(4, 0)
     use(order[3])
@@ -261,6 +278,8 @@
     A.step(4, 1)
     use(order[4])
     product(4)
+    out_merge(1)
+    out_merge(2)
     for c in pushes:
         c.wait_recv()
     hand_kv = remote(kv.at[r], kv.at[r], kp_sem.at[0], kp_sem.at[1], partner)
@@ -302,6 +321,8 @@
     product(5)
     product(6)
     product(7)
+    out_merge(3)
+    out_merge(4)
     hand_kv.wait_recv()
 
     def first(wp):
@@ -362,6 +383,9 @@
     nacc[...] = jnp.zeros_like(nacc)
 
     E.second()
+    out_merge(5)
+    out_merge(6)
+    out_merge(7)
 
     def key_sums():
         kacc[...] = S[w, xl].astype(jnp.float32)
@@ -397,16 +421,16 @@
         e_hands[k].wait_recv()
         for x in range(2):
             weight = wq[:, aligned(2 * at + x, QB)]
-            far = (((2 * at + x) // 3) // 4 + w // 4) % 2
+            far = across((2 * at + x) // 3)
             for h in range(2):
                 nacc[h] += dot(QF[h, at, x], weight, NT)
             total = dot(N[far, 0:QB, :], QF[0, at, x], TN) + dot(N[far, QB:512, :], QF[1, at, x], TN)
             F[4 * at + 2 * x] = total[:, 0:128].astype(low)
             F[4 * at + 2 * x + 1] = total[:, 128:256].astype(low)
 
-            @pl.when((2 * at + x) // 3 != w)
+            @pl.when(far == 1)
             def _():
-                two(2 * at + x).start()
+                two_cross(2 * at + x).start()
 
     def process_kv(k):
         at = v_order[k]
@@ -414,39 +438,74 @@
         for x in range(2):
             spot = 32 + 8 * x + at
             weight = wq[:, aligned(spot, 128)]
-            far = ((spot // 6) // 4 + w // 4) % 2
+            far = across(spot // 6)
             for h in range(2):
                 nacc[h] += dot(KF[h, at, x], weight, NT)
             total = dot(N[far, 0:QB, :], KF[0, at, x], TN) + dot(N[far, QB:512, :], KF[1, at, x], TN)
             F[spot] = total.astype(low)
 
-            @pl.when(spot // 6 != w)
+            @pl.when(far == 1)
+            def _():
+                one_cross(spot).start()
+
+    def two_cross(tp):
+        ref = pl.ds(2 * tp, 2)
+        return remote(F.at[ref], FX.at[ref], f_send.at[2 * tp], fx_recv.at[2 * tp], outer)
+
+    def one_cross(spot):
+        return remote(F.at[spot], FX.at[spot], f_send.at[spot], fx_recv.at[spot], outer)
+
+    def two(tp):
+        return remote(
+            F.at[pl.ds(2 * tp, 2)], FR.at[side, pl.ds(2 * (tp % 3), 2)],
+            f_send.at[2 * tp], f_recv.at[side, 2 * (tp % 3)], {"wide": tp // 3},
+        )
+
+    def one(spot):
+        return remote(
+            F.at[spot], FR.at[side, spot % 6], f_send.at[spot], f_recv.at[side, spot % 6],
+            {"wide": spot // 6},
+        )
+
+    def two_in(sy, j):
+        return remote(
+            F.at[pl.ds(6 * w + 2 * j, 2)], FR.at[sy, pl.ds(2 * j, 2)],
+            f_send.at[6 * w + 2 * j], f_recv.at[sy, 2 * j], {"wide": (w // 4) * 4 + sy},
+        )
+
+    def one_in(sy, j):
+        return remote(
+            F.at[6 * w + j], FR.at[sy, j], f_send.at[6 * w + j], f_recv.at[sy, j],
+            {"wide": (w // 4) * 4 + sy},
+        )
+
+    def merge(k):
+        for x in range(2):
+            tp = 2 * e_order[k] + x
+
+            @pl.when(across(tp // 3) == 0)
+            def _():
+                two_cross(tp).wait_recv()
+                for j in range(2):
+                    both = F[2 * tp + j].astype(jnp.float32) + FX[2 * tp + j].astype(jnp.float32)
+                    F[2 * tp + j] = both.astype(low)
+
+            @pl.when((across(tp // 3) == 0) & (tp // 3 != w))
+            def _():
+                two(tp).start()
+
+    def merge_kv(k):
+        for x in range(2):
+            spot = 32 + 8 * x + v_order[k]
+
+            @pl.when(across(spot // 6) == 0)
+            def _():
+                one_cross(spot).wait_recv()
+                F[spot] = (F[spot].astype(jnp.float32) + FX[spot].astype(jnp.float32)).astype(low)
+
+            @pl.when((across(spot // 6) == 0) & (spot // 6 != w))
             def _():
                 one(spot).start()
-
-    def peer(wp):
-        far = (wp // 4 + w // 4) % 2
-        return {"wide": wp, "tp": z * 2 + (xl + far) % 2}
-
-    def two(tp):
-        return remote(
-            F.at[pl.ds(2 * tp, 2)], FR.at[w, pl.ds(2 * (tp % 3), 2)],
-            f_send.at[2 * tp], f_recv.at[w, 2 * (tp % 3)], peer(tp // 3),
-        )
-
-    def one(spot):
-        return remote(
-            F.at[spot], FR.at[w, spot % 6], f_send.at[spot], f_recv.at[w, spot % 6], peer(spot // 6)
-        )
-
-    def two_in(ws, j):
-        return remote(
-            F.at[pl.ds(6 * w + 2 * j, 2)], FR.at[ws, pl.ds(2 * j, 2)],
-            f_send.at[6 * w + 2 * j], f_recv.at[ws, 2 * j], peer(ws),
-        )
-
-    def one_in(ws, j):
-        return remote(F.at[6 * w + j], FR.at[ws, j], f_send.at[6 * w + j], f_recv.at[ws, j], peer(ws))
 
     E.step(1, 0)
     lend_n.wait_recv()
@@ -467,6 +526,7 @@
     v_whole(0)
     E.step(3, 0)
     process(1)
+    merge(0)
     E.step(3, 1)
     V.step(2, 0)
     V.step(2, 1)
@@ -476,73 +536,86 @@
     process_kv(0)
     e_whole(2)
     v_whole(1)
+    merge(1)
     E.step(4, 0)
     process(3)
+    merge(2)
     E.step(4, 1)
     V.step(3, 0)
     V.step(3, 1)
     process(4)
+    merge_kv(0)
     E.step(4, 2)
     V.step(3, 2)
     process_kv(1)
     process_kv(2)
+    merge(3)
     e_whole(3)
     v_whole(2)
     process(5)
     process(6)
+    merge(4)
     e_whole(4)
     V.step(4, 0)
     V.step(4, 1)
     V.step(4, 2)
     process_kv(3)
     process_kv(4)
+    merge_kv(1)
+    merge_kv(2)
     process(7)
+    merge(5)
+    merge(6)
     v_whole(3)
     v_whole(4)
     process_kv(5)
     process_kv(6)
+    merge_kv(3)
+    merge_kv(4)
     process_kv(7)
+    merge(7)
+    merge_kv(5)
+    merge_kv(6)
+    merge_kv(7)
 
     for h in range(2):
         ng_out[h * QB:(h + 1) * QB, :] = nacc[h].astype(low)
 
-    OR[w] = OP[w]
-
-    @pl.loop(0, 8)
-    def _(ws):
-        @pl.when(ws != w)
-        def _():
-            far = (ws // 4 + w // 4) % 2
+    OR[side] = OP[w]
+
+    @pl.loop(0, 4)
+    def _(sy):
+        @pl.when(sy != side)
+        def _():
             remote(
-                OP.at[w], OR.at[ws], o_send.at[w], o_recv.at[ws],
-                {"wide": ws, "tp": z * 2 + (xl + far) % 2},
+                OP.at[w], OR.at[sy], o_send.at[w], o_recv.at[sy], {"wide": (w // 4) * 4 + sy}
             ).wait_recv()
 
     total = OR[0].astype(jnp.float32)
-    for ws in range(1, 8):
-        total += OR[ws].astype(jnp.float32)
+    for sy in range(1, 4):
+        total += OR[sy].astype(jnp.float32)
     ow_out[...] = total.astype(low)
 
-    FR[w] = F[pl.ds(6 * w, 6)]
-
-    @pl.loop(0, 8)
-    def _(ws):
-        @pl.when(ws != w)
+    FR[side] = F[pl.ds(6 * w, 6)]
+
+    @pl.loop(0, 4)
+    def _(sy):
+        @pl.when(sy != side)
         def _():
             for j in range(3):
                 @pl.when((w < 5) | ((w == 5) & (j == 0)))
                 def _():
-                    two_in(ws, j).wait_recv()
+                    two_in(sy, j).wait_recv()
 
             for j in range(6):
                 @pl.when((w > 5) | ((w == 5) & (j > 1)))
                 def _():
-                    one_in(ws, j).wait_recv()
+                    one_in(sy, j).wait_recv()
 
     for j in range(6):
         total = FR[0, j].astype(jnp.float32)
-        for ws in range(1, 8):
-            total += FR[ws, j].astype(jnp.float32)
+        for sy in range(1, 4):
+            total += FR[sy, j].astype(jnp.float32)
         gw_out[:, j * 128:(j + 1) * 128] = total.astype(low)
 
     for c in sends + pushes + hands + e_hands + v_hands:
@@ -574,6 +647,38 @@
         @pl.when((32 + tp) // 6 != w)
         def _():
             one(32 + tp).wait_send()
+
+
+def emit_kernel(a, b, c, a_out, b_out, c_out, a_in, b_in, c_in, sem):
+    loads = [
+        pltpu.make_async_copy(x, y, sem.at[0, k])
+        for k, (x, y) in enumerate(((a, a_in), (b, b_in), (c, c_in)))
+    ]
+    stores = [
+        pltpu.make_async_copy(x, y, sem.at[1, k])
+        for k, (x, y) in enumerate(((a_in, a_out), (b_in, b_out), (c_in, c_out)))
+    ]
+    for copy in loads:
+        copy.start()
+    for load, store in zip(loads, stores):
+        load.wait()
+        store.start()
+    for copy in stores:
+        copy.wait()
+
+
+def emit(arrays):
+    hbm = pl.BlockSpec(memory_space=pltpu.HBM)
+    return pl.pallas_call(
+        emit_kernel,
+        name="emit",
+        out_shape=tuple(jax.ShapeDtypeStruct(a.shape, a.dtype) for a in arrays),
+        in_specs=[hbm] * 3,
+        out_specs=(hbm,) * 3,
+        scratch_shapes=[pltpu.VMEM(a.shape, a.dtype) for a in arrays] + [pltpu.SemaphoreType.DMA((2, 3))],
+        compiler_params=pltpu.CompilerParams(vmem_limit_bytes=60 * 1024 * 1024),
+        cost_estimate=pl.CostEstimate(flops=1_000_000, bytes_accessed=1_000_000, transcendentals=0),
+    )(*arrays)
 
 
 def local(
@@ -584,7 +689,7 @@
     dma = pltpu.SemaphoreType.DMA
     low, wide = jnp.bfloat16, jnp.float32
     ring = [dma((2, 4, 3)), dma((2, 4, 3)), dma((9,)), dma((9,)), dma((8,)), dma((8,))]
-    return pl.pallas_call(
+    done = pl.pallas_call(
         whole_kernel,
         name="layer",
         out_shape=(
@@ -602,6 +707,7 @@
             pltpu.VMEM((2, 512, QB), low),
             pltpu.VMEM((8, QB, QB), low),
             pltpu.VMEM((8, QB, QB), low),
+            pltpu.VMEM((4, QB, QB), low),
             pltpu.VMEM((QB, QB), wide),
             pltpu.VMEM((2, 8, 512, 128), low),
             pltpu.VMEM((QB, QB), low),
@@ -617,16 +723,17 @@
             pltpu.VMEM((8, 2, QB, 128), low),
             pltpu.VMEM((8, 2, QB, 128), low),
             pltpu.VMEM((48, 128, 128), low),
-            pltpu.VMEM((8, 6, 128, 128), low),
+            pltpu.VMEM((48, 128, 128), low),
+            pltpu.VMEM((4, 6, 128, 128), low),
             pltpu.VMEM((2, 512, 128), low),
             pltpu.VMEM((128, 6144), low),
             pltpu.VMEM((2, QB, 128), wide),
             pltpu.VMEM((QB, 128), wide),
             dma((9,)), dma((2,)), dma((7,)), dma((7,)), dma((2,)), dma((2,)), dma((2,)), dma((2,)),
-            dma((8,)), dma((8,)),
+            dma((8,)), dma((8,)), dma((4,)),
         ]
         + ring * 3
-        + [dma((8,)), dma((8,)), dma((8, 2)), dma((8, 2)), dma((48,)), dma((8, 6))],
+        + [dma((8,)), dma((8,)), dma((8, 2)), dma((8, 2)), dma((48,)), dma((48,)), dma((4, 6))],
         compiler_params=pltpu.CompilerParams(
             collective_id=0, has_side_effects=True, vmem_limit_bytes=60 * 1024 * 1024
         ),
@@ -637,6 +744,7 @@
         normed, queries, keys, values, attn_out, row_logsumexp, out_grad, out_weight, qkv_weight,
         documents.reshape(32, 128),
     )
+    return emit(done)
 
 
 def solution(mesh):

time: 105 us -> 105 us (level)
  the two profiles are of different devices: /device:TPU:17 before, /device:TPU:23 now
where the time goes in v4:
time: 105 us; the launch traced here: 103 us
  Pallas kernels  103 us (98%)
    pallas_call x1, Pallas kernels, local(): pl.pallas_call(whole_kernel, name='layer', out_shape=(jax.ShapeDtypeStruc...  101 us

profile of v4, /device:TPU:23, one launch (start us, length us, event | category | flops | bytes accessed | tf_op | source)
XLA Modules:
  0.0 103.3 jit_solution(7351005363177726619)
XLA Ops:
  0.6 100.8 %layer.1 = (bf16[512,128]{1,0:T(8,128)(2,1)}, bf16[256,256]{1,0:T(8,128)(2,1)}, bf16[128,768]{1,0:T(8,128)(2,1)}) custom-call(bf16[512,128]{1,0:T(8,128)(2,1)} %normed.1, bf16[512,256]{1,0:T(8,128)(2,1)} %queries.1, bf16[512,1024]{1,0:T(8,128)(2,1)} %keys.1, bf16[512,1024]{1,0:T(8,128)(2,1)} %values.1, bf16[512,256]{1,0:T(8,128)(2,1)} %ao.1, ...), custom_call_target="tpu_custom_call" | custom-call | flops 10000000000 | bytes 40000000 | tf_op jit(solution)/shard_map/layer/pallas_call | solution.py:692
  101.5 1.8 %emit.1 = (bf16[512,128]{1,0:T(8,128)(2,1)}, bf16[256,256]{1,0:T(8,128)(2,1)}, bf16[128,768]{1,0:T(8,128)(2,1)}) custom-call(bf16[512,128]{1,0:T(8,128)(2,1)} %get-tuple-element.6.a, bf16[256,256]{1,0:T(8,128)(2,1)} %get-tuple-element.7.b, bf16[128,768]{1,0:T(8,128)(2,1)} %get-tuple-element.8.c), custom_call_target="tpu_custom_call" | custom-call | flops 1000000 | bytes 1000000 | tf_op jit(solution)/shard_map/emit/pallas_call | solution.py:672

commit v5 on v4

--- a/solution.py
+++ b/solution.py
@@ -346,8 +346,21 @@
         S[wp, 0] = both[:, 0:128]
         S[wp, 1] = both[:, 128:256]
 
+    def reduce_pair(wp):
+        pair_sum(wp)
+
+        @pl.when(wp == w)
+        def _():
+            second(w, 1 - xl).start()
+
+        @pl.when(wp != w)
+        def _():
+            second(wp, 0).start()
+            second(wp, 1).start()
+
     @pl.loop(0, w + 1)
-    def _(i):
+    def _(n):
+        i = w - n
         k_rows = kv[0, i]
         v_rows = kv[1, i]
         scores = dot(k_rows, q2[...], NT)
@@ -364,17 +377,14 @@
             dkv[i, h, :, 128:256] = dv[h * QB:(h + 1) * QB, :]
         first(i).start()
 
-        @pl.when(i > 0)
-        def _():
-            pair_sum(i - 1)
-            second(i - 1, 0).start()
-            second(i - 1, 1).start()
+        @pl.when(n > 0)
+        def _():
+            reduce_pair(i + 1)
 
     for h in range(2):
         dqb[:, h * 128:(h + 1) * 128] = (dq[pl.ds(h * QB, QB), :] * SCALE).astype(low)
     QF[r, z, xl] = dqb[...]
-    pair_sum(w)
-    second(w, 1 - xl).start()
+    reduce_pair(0 * w)
 
     E = Gather(lambda at, x, row, n: QF.at[r, at, x, pl.ds(row, n), :], ez_s, ez_r, ex_s, ex_r)
     V = Gather(lambda at, x, row, n: KF.at[r, at, x, pl.ds(row, n), :], vz_s, vz_r, vx_s, vx_r)

time: 105 us -> 106 us (level)
  no operation moved by 1% of the time
where the time goes in v5:
time: 106 us; the launch traced here: 104 us
  Pallas kernels  103 us (97%)
    pallas_call x1, Pallas kernels, local(): pl.pallas_call(whole_kernel, name='layer', out_shape=(jax.ShapeDtypeStruc...  101 us

profile of v5, /device:TPU:23, one launch (start us, length us, event | category | flops | bytes accessed | tf_op | source)
XLA Modules:
  0.0 103.6 jit_solution(15778049152923164765)
XLA Ops:
  0.6 101.1 %layer.1 = (bf16[512,128]{1,0:T(8,128)(2,1)}, bf16[256,256]{1,0:T(8,128)(2,1)}, bf16[128,768]{1,0:T(8,128)(2,1)}) custom-call(bf16[512,128]{1,0:T(8,128)(2,1)} %normed.1, bf16[512,256]{1,0:T(8,128)(2,1)} %queries.1, bf16[512,1024]{1,0:T(8,128)(2,1)} %keys.1, bf16[512,1024]{1,0:T(8,128)(2,1)} %values.1, bf16[512,256]{1,0:T(8,128)(2,1)} %ao.1, ...), custom_call_target="tpu_custom_call" | custom-call | flops 10000000000 | bytes 40000000 | tf_op jit(solution)/shard_map/layer/pallas_call | solution.py:702
  101.8 1.8 %emit.1 = (bf16[512,128]{1,0:T(8,128)(2,1)}, bf16[256,256]{1,0:T(8,128)(2,1)}, bf16[128,768]{1,0:T(8,128)(2,1)}) custom-call(bf16[512,128]{1,0:T(8,128)(2,1)} %get-tuple-element.6.a, bf16[256,256]{1,0:T(8,128)(2,1)} %get-tuple-element.7.b, bf16[128,768]{1,0:T(8,128)(2,1)} %get-tuple-element.8.c), custom_call_target="tpu_custom_call" | custom-call | flops 1000000 | bytes 1000000 | tf_op jit(solution)/shard_map/emit/pallas_call | solution.py:682

commit v6 on v5

--- a/solution.py
+++ b/solution.py
@@ -393,9 +393,6 @@
     nacc[...] = jnp.zeros_like(nacc)
 
     E.second()
-    out_merge(5)
-    out_merge(6)
-    out_merge(7)
 
     def key_sums():
         kacc[...] = S[w, xl].astype(jnp.float32)
@@ -454,40 +451,45 @@
             total = dot(N[far, 0:QB, :], KF[0, at, x], TN) + dot(N[far, QB:512, :], KF[1, at, x], TN)
             F[spot] = total.astype(low)
 
-            @pl.when(far == 1)
+            @pl.when(spot // 6 != w)
             def _():
-                one_cross(spot).start()
+                one(spot).start()
 
     def two_cross(tp):
         ref = pl.ds(2 * tp, 2)
         return remote(F.at[ref], FX.at[ref], f_send.at[2 * tp], fx_recv.at[2 * tp], outer)
 
-    def one_cross(spot):
-        return remote(F.at[spot], FX.at[spot], f_send.at[spot], fx_recv.at[spot], outer)
-
     def two(tp):
         return remote(
-            F.at[pl.ds(2 * tp, 2)], FR.at[side, pl.ds(2 * (tp % 3), 2)],
-            f_send.at[2 * tp], f_recv.at[side, 2 * (tp % 3)], {"wide": tp // 3},
+            F.at[pl.ds(2 * tp, 2)], FR.at[w, pl.ds(2 * (tp % 3), 2)],
+            f_send.at[2 * tp], f_recv.at[w, 2 * (tp % 3)], {"wide": tp // 3},
         )
+
+    def peer(wp):
+        return {"wide": wp, "tp": z * 2 + (xl + across(wp)) % 2}
 
     def one(spot):
         return remote(
-            F.at[spot], FR.at[side, spot % 6], f_send.at[spot], f_recv.at[side, spot % 6],
-            {"wide": spot // 6},
+            F.at[spot], FR.at[w, spot % 6], f_send.at[spot], f_recv.at[w, spot % 6], peer(spot // 6)
         )
 
-    def two_in(sy, j):
+    def two_in(ws, j):
         return remote(
-            F.at[pl.ds(6 * w + 2 * j, 2)], FR.at[sy, pl.ds(2 * j, 2)],
-            f_send.at[6 * w + 2 * j], f_recv.at[sy, 2 * j], {"wide": (w // 4) * 4 + sy},
+            F.at[pl.ds(6 * w + 2 * j, 2)], FR.at[ws, pl.ds(2 * j, 2)],
+            f_send.at[6 * w + 2 * j], f_recv.at[ws, 2 * j], {"wide": ws},
         )
 
-    def one_in(sy, j):
-        return remote(
-            F.at[6 * w + j], FR.at[sy, j], f_send.at[6 * w + j], f_recv.at[sy, j],
-            {"wide": (w // 4) * 4 + sy},
-        )
+    def one_in(ws, j):
+        return remote(F.at[6 * w + j], FR.at[ws, j], f_send.at[6 * w + j], f_recv.at[ws, j], peer(ws))
+
+    for ws in range(8):
+        @pl.when((across(ws) == 1) & (w < 6))
+        def _():
+            FR[ws, 0:2] = jnp.zeros((2, 128, 128), low)
+
+        @pl.when((across(ws) == 1) & (w < 5))
+        def _():
+            FR[ws, 2:6] = jnp.zeros((4, 128, 128), low)
 
     def merge(k):
         for x in range(2):
@@ -504,31 +506,21 @@
             def _():
                 two(tp).start()
 
-    def merge_kv(k):
-        for x in range(2):
-            spot = 32 + 8 * x + v_order[k]
-
-            @pl.when(across(spot // 6) == 0)
-            def _():
-                one_cross(spot).wait_recv()
-                F[spot] = (F[spot].astype(jnp.float32) + FX[spot].astype(jnp.float32)).astype(low)
-
-            @pl.when((across(spot // 6) == 0) & (spot // 6 != w))
-            def _():
-                one(spot).start()
-
+    key_sums()
+    V.start()
     E.step(1, 0)
     lend_n.wait_recv()
     E.step(1, 1)
-    key_sums()
-    V.start()
+    out_merge(5)
+    out_merge(6)
+    out_merge(7)
+    V.second()
     E.step(1, 2)
-    V.second()
     e_whole(0)
+    V.step(1, 0)
     E.step(2, 0)
+    V.step(1, 1)
     E.step(2, 1)
-    V.step(1, 0)
-    V.step(1, 1)
     process(0)
     E.step(2, 2)
     V.step(1, 2)
@@ -554,7 +546,6 @@
     V.step(3, 0)
     V.step(3, 1)
     process(4)
-    merge_kv(0)
     E.step(4, 2)
     V.step(3, 2)
     process_kv(1)
@@ -571,8 +562,6 @@
     V.step(4, 2)
     process_kv(3)
     process_kv(4)
-    merge_kv(1)
-    merge_kv(2)
     process(7)
     merge(5)
     merge(6)
@@ -580,13 +569,8 @@
     v_whole(4)
     process_kv(5)
     process_kv(6)
-    merge_kv(3)
-    merge_kv(4)
     process_kv(7)
     merge(7)
-    merge_kv(5)
-    merge_kv(6)
-    merge_kv(7)
 
     for h in range(2):
         ng_out[h * QB:(h + 1) * QB, :] = nacc[h].astype(low)
@@ -606,26 +590,26 @@
         total += OR[sy].astype(jnp.float32)
     ow_out[...] = total.astype(low)
 
-    FR[side] = F[pl.ds(6 * w, 6)]
-
-    @pl.loop(0, 4)
-    def _(sy):
-        @pl.when(sy != side)
+    FR[w] = F[pl.ds(6 * w, 6)]
+
+    @pl.loop(0, 8)
+    def _(ws):
+        @pl.when(ws != w)
         def _():
             for j in range(3):
-                @pl.when((w < 5) | ((w == 5) & (j == 0)))
+                @pl.when((across(ws) == 0) & ((w < 5) | ((w == 5) & (j == 0))))
                 def _():
-                    two_in(sy, j).wait_recv()
+                    two_in(ws, j).wait_recv()
 
             for j in range(6):
                 @pl.when((w > 5) | ((w == 5) & (j > 1)))
                 def _():
-                    one_in(sy, j).wait_recv()
+                    one_in(ws, j).wait_recv()
 
     for j in range(6):
         total = FR[0, j].astype(jnp.float32)
-        for sy in range(1, 4):
-            total += FR[sy, j].astype(jnp.float32)
+        for ws in range(1, 8):
+            total += FR[ws, j].astype(jnp.float32)
         gw_out[:, j * 128:(j + 1) * 128] = total.astype(low)
 
     for c in sends + pushes + hands + e_hands + v_hands:
@@ -734,7 +718,7 @@
             pltpu.VMEM((8, 2, QB, 128), low),
             pltpu.VMEM((48, 128, 128), low),
             pltpu.VMEM((48, 128, 128), low),
-            pltpu.VMEM((4, 6, 128, 128), low),
+            pltpu.VMEM((8, 6, 128, 128), low),
             pltpu.VMEM((2, 512, 128), low),
             pltpu.VMEM((128, 6144), low),
             pltpu.VMEM((2, QB, 128), wide),
@@ -743,7 +727,7 @@
             dma((8,)), dma((8,)), dma((4,)),
         ]
         + ring * 3
-        + [dma((8,)), dma((8,)), dma((8, 2)), dma((8, 2)), dma((48,)), dma((48,)), dma((4, 6))],
+        + [dma((8,)), dma((8,)), dma((8, 2)), dma((8, 2)), dma((48,)), dma((48,)), dma((8, 6))],
         compiler_params=pltpu.CompilerParams(
             collective_id=0, has_side_effects=True, vmem_limit_bytes=60 * 1024 * 1024
         ),

time: 106 us -> 107 us (level); the launches traced: 104 us -> 106 us
  Pallas kernels: 103 us -> 106 us
    pallas_call x1, Pallas kernels: 101 us -> 104 us  [local(): pl.pallas_call(whole_kernel, name='layer', out_shape=(jax.ShapeDtypeStruc...]
where the time goes in v6:
time: 107 us; the launch traced here: 106 us
  Pallas kernels  106 us (99%)
    pallas_call x1, Pallas kernels, local(): pl.pallas_call(whole_kernel, name='layer', out_shape=(jax.ShapeDtypeStruc...  104 us

profile of v6, /device:TPU:23, one launch (start us, length us, event | category | flops | bytes accessed | tf_op | source)
XLA Modules:
  0.0 106.2 jit_solution(10661767113055156069)
XLA Ops:
  0.6 103.8 %layer.1 = (bf16[512,128]{1,0:T(8,128)(2,1)}, bf16[256,256]{1,0:T(8,128)(2,1)}, bf16[128,768]{1,0:T(8,128)(2,1)}) custom-call(bf16[512,128]{1,0:T(8,128)(2,1)} %normed.1, bf16[512,256]{1,0:T(8,128)(2,1)} %queries.1, bf16[512,1024]{1,0:T(8,128)(2,1)} %keys.1, bf16[512,1024]{1,0:T(8,128)(2,1)} %values.1, bf16[512,256]{1,0:T(8,128)(2,1)} %ao.1, ...), custom_call_target="tpu_custom_call" | custom-call | flops 10000000000 | bytes 40000000 | tf_op jit(solution)/shard_map/layer/pallas_call | solution.py:686
  104.4 1.8 %emit.1 = (bf16[512,128]{1,0:T(8,128)(2,1)}, bf16[256,256]{1,0:T(8,128)(2,1)}, bf16[128,768]{1,0:T(8,128)(2,1)}) custom-call(bf16[512,128]{1,0:T(8,128)(2,1)} %get-tuple-element.6.a, bf16[256,256]{1,0:T(8,128)(2,1)} %get-tuple-element.7.b, bf16[128,768]{1,0:T(8,128)(2,1)} %get-tuple-element.8.c), custom_call_target="tpu_custom_call" | custom-call | flops 1000000 | bytes 1000000 | tf_op jit(solution)/shard_map/emit/pallas_call | solution.py:666
